TPU v7x, 32 devices: a whole 2x2x4 slice. The times are simulated.
32 devices in a mesh: dp: 2 (over core), gx: 4 (over y, x), gy: 4 (over z).
Axes of the slice: x: 2, y: 2, z: 4, core: 2. Of those that a mesh axis runs over, the one named last changes fastest.
Arguments:
- volume: bfloat16 [2, 4, 8, 32, 128], P('dp', None, 'gx', 'gy'), may hold values from -6 to 6
- targets: float32 [2, 4], P('dp'), may hold values from -4 to 4
- conv1_w: bfloat16 [27, 128], replicated, may hold values from -0.625 to 0.625
- conv1_b: float32 [32], replicated, may hold values from -3 to 3
- conv2_w: bfloat16 [27, 2048], replicated, may hold values from -0.21875 to 0.21875
- conv2_b: float32 [64], replicated, may hold values from -3 to 3
- head_w: float32 [64, 4], replicated, may hold values from -2 to 2
- head_b: float32 [4], replicated, may hold values from -4 to 4
- dir1: float32 [27, 128], replicated, may hold values from -6 to 6
- dir2: float32 [27, 2048], replicated, may hold values from -1.2 to 1.2
- dir_head: float32 [64, 4], replicated, may hold values from -6 to 6
Outputs:
- next1: float32 [27, 128], replicated
- next2: float32 [27, 2048], replicated
- next_head: float32 [64, 4], replicated
- rayleigh: float32 [], replicated
- curvature_field: float32 [2, 32, 8, 32, 128], P('dp', None, 'gx', 'gy')
All inputs are finite; a program needn't handle non-finite values.
Results may differ from a plain program's by a relative error of at most 0.0051.
Values may be sent and summed in bfloat16 or wider, within the bound.
A program may use at most 128 MiB of HBM per device.

v0:
```python
import jax
import jax.numpy as jnp
from jax import lax
from jax.sharding import PartitionSpec as P

C0 = 4
C1 = 32
C2 = 64


def extended(cells, sides, width):
    for axis, dim in sides:
        count = lax.axis_size(axis)
        ends = count - 1
        head = lax.slice_in_dim(cells, 0, width, axis=dim)
        tail = lax.slice_in_dim(cells, cells.shape[dim] - width, cells.shape[dim], axis=dim)
        cells = jnp.concatenate(
            [
                lax.ppermute(tail, axis, [(i, (i + 1) % count) for i in range(ends)]),
                cells,
                lax.ppermute(head, axis, [((i + 1) % count, i) for i in range(ends)]),
            ],
            axis=dim,
        )
    return cells


def silu_parts(z):
    s = jax.nn.sigmoid(z)
    return (z * s, s * (1.0 + z * (1.0 - s)), s * (1.0 - s) * (2.0 + z * (1.0 - 2.0 * s)))


def as_kernel(flat, outer, inner):
    return flat.reshape(3, 3, 3, outer, inner).transpose(3, 4, 0, 1, 2)


def pad_depth(a):
    return jnp.pad(a, ((0, 0), (0, 0), (0, 0), (0, 0), (1, 1)))


def convolve(padded, kernel):
    return lax.conv_general_dilated(
        pad_depth(padded),
        kernel,
        (1, 1, 1),
        "VALID",
        dimension_numbers=("NCDHW", "OIDHW", "NCDHW"),
        preferred_element_type=jnp.float32,
    )


def flipped(kernel):
    return jnp.flip(kernel, (2, 3, 4)).transpose(1, 0, 2, 3, 4)


def correlate(padded, grads):
    wide = pad_depth(padded)
    sx, sy, sz = (grads.shape[2], grads.shape[3], grads.shape[4])
    pieces = []
    for a in range(3):
        for b in range(3):
            for c in range(3):
                window = wide[:, :, a : a + sx, b : b + sy, c : c + sz]
                pieces.append(
                    jnp.einsum("bixyz,boxyz->oi", window, grads, preferred_element_type=jnp.float32)
                )
    stacked = jnp.stack(pieces, axis=0)
    return stacked.reshape(27, grads.shape[1] * padded.shape[1])


def spread(vector):
    return vector[:, :, None, None, None]


def per_device(
    volume, targets, conv1_w, conv1_b, conv2_w, conv2_b, head_w, head_b, dir1, dir2, dir_head
):
    high = lax.Precision.HIGHEST
    weight1 = as_kernel(conv1_w, C1, C0)
    weight2 = as_kernel(conv2_w, C2, C1)
    kern1 = as_kernel(dir1.astype(jnp.bfloat16), C1, C0)
    kern2 = as_kernel(dir2.astype(jnp.bfloat16), C2, C1)
    depth, height = (volume.shape[2], volume.shape[3])
    padded_in = extended(volume, (("gx", 2), ("gy", 3)), 1)
    z1 = convolve(padded_in, weight1) + conv1_b[None, :, None, None, None]
    t1 = convolve(padded_in, kern1)
    act1, slope1, bend1 = silu_parts(z1)
    a1 = act1.astype(jnp.bfloat16)
    ta1 = (slope1 * t1).astype(jnp.bfloat16)
    pa1 = extended(a1, (("gx", 2), ("gy", 3)), 1)
    pta1 = extended(ta1, (("gx", 2), ("gy", 3)), 1)
    z2 = convolve(pa1, weight2) + conv2_b[None, :, None, None, None]
    t2 = convolve(pta1, weight2) + convolve(pa1, kern2)
    act2, slope2, bend2 = silu_parts(z2)
    width = z2.shape[4]
    cells = depth * lax.axis_size("gx") * height * lax.axis_size("gy") * width
    sums = lax.psum(
        (jnp.sum(act2, axis=(2, 3, 4)), jnp.sum(slope2 * t2, axis=(2, 3, 4))), ("gx", "gy")
    )
    pooled = sums[0] / cells
    tpooled = sums[1] / cells
    batch = volume.shape[0] * lax.axis_size("dp")
    outputs = jnp.dot(pooled, head_w, precision=high) + head_b
    toutputs = jnp.dot(tpooled, head_w, precision=high) + jnp.dot(pooled, dir_head, precision=high)
    dy = (outputs - targets) / batch
    tdy = toutputs / batch
    leader = ((lax.axis_index("gx") == 0) & (lax.axis_index("gy") == 0)).astype(jnp.float32)
    hd = leader * (jnp.dot(tpooled.T, dy, precision=high) + jnp.dot(pooled.T, tdy, precision=high))
    dpool = jnp.dot(dy, head_w.T, precision=high) / cells
    tdpool = (
        jnp.dot(tdy, head_w.T, precision=high) + jnp.dot(dy, dir_head.T, precision=high)
    ) / cells
    g2 = (slope2 * spread(dpool)).astype(jnp.bfloat16)
    tg2 = (bend2 * t2 * spread(dpool) + slope2 * spread(tdpool)).astype(jnp.bfloat16)
    back_w = flipped(weight2)
    back_k = flipped(kern2)
    joined = extended(jnp.stack((g2, tg2)), (("gx", 3), ("gy", 4)), 1)
    pg2, ptg2 = (joined[0], joined[1])
    da1 = convolve(pg2, back_w)
    tda1 = convolve(ptg2, back_w) + convolve(pg2, back_k)
    tg1 = (bend1 * t1 * da1 + slope1 * tda1).astype(jnp.bfloat16)
    h1 = correlate(padded_in, tg1)
    h2 = correlate(pa1, tg2) + correlate(pta1, g2)
    h1, h2, hd = lax.psum((h1, h2, hd), ("dp", "gx", "gy"))
    field = tda1 * cells
    quad = jnp.sum(dir1 * h1) + jnp.sum(dir2 * h2) + jnp.sum(dir_head * hd)
    length = jnp.sum(dir1 * dir1) + jnp.sum(dir2 * dir2) + jnp.sum(dir_head * dir_head)
    nrm = jnp.sqrt(jnp.sum(h1 * h1) + jnp.sum(h2 * h2) + jnp.sum(hd * hd) + 1e-06)
    return (h1 / nrm, h2 / nrm, hd / nrm, quad / length, field)


def solution(mesh):
    return jax.shard_map(
        per_device,
        mesh=mesh,
        in_specs=(
            P("dp", None, "gx", "gy", None),
            P("dp", None),
            P(),
            P(),
            P(),
            P(),
            P(),
            P(),
            P(),
            P(),
            P(),
        ),
        out_specs=(P(), P(), P(), P(), P("dp", None, "gx", "gy", None)),
        check_vma=False,
    )
```

profile of v0, /device:TPU:0, one launch (start us, length us, event | category | flops | bytes accessed | tf_op | source)
XLA Modules:
  0.0 376.5 jit_solution(5744117732220031743)
XLA Ops:
  8.0 4.9 %collective-permute-start = (bf16[1,4,1,8,128]{4,1,3,2,0:T(4,128)(2,1)S(1)}, bf16[1,4,1,8,128]{4,1,3,2,0:T(4,128)(2,1)S(1)}, u32[]{:S(2)}, u32[]{:S(2)}) collective-permute-start(bf16[1,4,1,8,128]{4,1,3,2,0:T(4,128)(2,1)S(1)} %get-tuple-element.60), channel_id=1, source_target_pairs={{0,4},{4,8},{8,12},{1,5},{5,9},{9,13},{2,6},{6,10},{10,14},{3,7},{... | collective-permute-start | bytes 24584 | tf_op jit(solution)/shard_map/ppermute | solution.py:19
  12.9 1.3 collective-permute-start.1
  15.0 3.5 collective-permute-done.1
  18.5 1.3 collective-permute-start.3
  19.8 4.5 %collective-permute-start.2 = (bf16[1,4,4,1,128]{4,1,3,2,0:T(4,128)(2,1)S(1)}, bf16[1,4,4,1,128]{4,1,3,2,0:T(4,128)(2,1)S(1)}, u32[]{:S(2)}, u32[]{:S(2)}) collective-permute-start(bf16[1,4,4,1,128]{4,1,3,2,0:T(4,128)(2,1)S(1)} %get-tuple-element.57), channel_id=1, source_target_pairs={{0,1},{1,2},{2,3},{4,5},{5,6},{6,7},{8,9},{9,10},{10,11},{12,13},{... | collective-permute-start | bytes 12296 | tf_op jit(solution)/shard_map/ppermute | solution.py:19
  24.3 2.0 reshape.567
  30.4 1.4 copy.299
  31.9 6.4 %fusion.38 = f32[2,8,8,17,32]{4,2,3,1,0:T(8,128)S(1)} fusion(bf16[3,3,3,32,4]{4,3,2,1,0:T(8,128)(2,1)S(1)} %reshape.565, f32[32]{0:T(128)S(1)} %copy-done.53, pred[8,17]{0,1:T(8,128)(4,1)S(1)} %copy-done.57, bf16[4,4,10,1,7,2]{4,0,5,2,1,3:T(4,128)(2,1)S(1)} %slice.473, bf16[4,4,10,1,8,17]{4,0,5,2,1,3:T(4,128)(2,1)S(1)} %copy.299), kind=kOutput, calls=%fused_computation.77 | convolution fusion | flops 15325696 | bytes 333704 | tf_op jit(solution)/shard_map/conv_general_dilated | solution.py:42
  38.3 7.7 %multiply_convert_fusion.1 = (bf16[2,8,8,17,32]{4,2,3,1,0:T(8,128)(2,1)S(1)}, bf16[2,8,8,17,32]{4,2,3,1,0:T(8,128)(2,1)S(1)}, f32[2,8,8,17,32]{4,2,3,1,0:T(8,128)}) fusion(f32[2,8,8,17,32]{4,2,3,1,0:T(8,128)S(1)} %fusion.38, bf16[3,3,3,32,4]{4,3,2,1,0:T(8,128)(2,1)S(1)} %reshape.566, bf16[4,4,10,1,7,2]{4,0,5,2,1,3:T(4,128)(2,1)S(1)} %slice.473, ...), kind=kOutput, calls=%fused_computation.95 | convolution fusion | flops 16022016 | bytes 890632 | tf_op jit(solution)/shard_map/conv_general_dilated | solution.py:42
  46.5 1.3 collective-permute-start.5
  48.4 4.9 %collective-permute-start.4 = (bf16[1,32,1,8,128]{4,1,3,2,0:T(8,128)(2,1)S(1)}, bf16[1,32,1,8,128]{4,1,3,2,0:T(8,128)(2,1)S(1)}, u32[]{:S(2)}, u32[]{:S(2)}) collective-permute-start(bf16[1,32,1,8,128]{4,1,3,2,0:T(8,128)(2,1)S(1)} %bitcast.755), channel_id=1, source_target_pairs={{0,4},{4,8},{8,12},{1,5},{5,9},{9,13},{2,6},{6,10},{10,14},{3,7},{... | collective-permute-start | bytes 196616 | tf_op jit(solution)/shard_map/ppermute | solution.py:19
  55.6 5.4 %collective-permute-start.8 = (bf16[1,32,1,8,128]{4,1,3,2,0:T(8,128)(2,1)S(1)}, bf16[1,32,1,8,128]{4,1,3,2,0:T(8,128)(2,1)S(1)}, u32[]{:S(2)}, u32[]{:S(2)}) collective-permute-start(bf16[1,32,1,8,128]{4,1,3,2,0:T(8,128)(2,1)S(1)} %bitcast.756), channel_id=1, source_target_pairs={{0,4},{4,8},{8,12},{1,5},{5,9},{9,13},{2,6},{6,10},{10,14},{3,7},{... | collective-permute-start | bytes 196616 | tf_op jit(solution)/shard_map/ppermute | solution.py:19
  61.2 1.3 collective-permute-start.7
  62.5 4.5 %collective-permute-start.6 = (bf16[1,32,4,1,128]{4,1,3,2,0:T(8,128)(2,1)S(1)}, bf16[1,32,4,1,128]{4,1,3,2,0:T(8,128)(2,1)S(1)}, u32[]{:S(2)}, u32[]{:S(2)}) collective-permute-start(bf16[1,32,4,1,128]{4,1,3,2,0:T(8,128)(2,1)S(1)} %get-tuple-element.55), channel_id=1, source_target_pairs={{0,1},{1,2},{2,3},{4,5},{5,6},{6,7},{8,9},{9,10},{10,11},{12,13},{... | collective-permute-start | bytes 98312 | tf_op jit(solution)/shard_map/ppermute | solution.py:19
  69.0 4.5 %collective-permute-start.10 = (bf16[1,32,4,1,128]{4,1,3,2,0:T(8,128)(2,1)}, bf16[1,32,4,1,128]{4,1,3,2,0:T(8,128)(2,1)S(1)}, u32[]{:S(2)}, u32[]{:S(2)}) collective-permute-start(bf16[1,32,4,1,128]{4,1,3,2,0:T(8,128)(2,1)} %get-tuple-element.53), channel_id=1, source_target_pairs={{0,1},{1,2},{2,3},{4,5},{5,6},{6,7},{8,9},{9,10},{10,11},{12,13},{... | collective-permute-start | bytes 98312 | tf_op jit(solution)/shard_map/ppermute | solution.py:19
  78.7 1.9 convolution_select_fusion.2
  80.7 1.9 fusion.37
  82.7 2.4 select_reduce_fusion
  85.1 39.3 %all-reduce.4 = (f32[1,64]{1,0:T(1,128)S(1)}, f32[1,64]{1,0:T(1,128)S(1)}) all-reduce(f32[1,64]{1,0:T(1,128)S(1)} %bitcast.760, f32[1,64]{1,0:T(1,128)S(1)} %bitcast.759), channel_id=1, replica_groups=mesh['dp'=2,'gx'=4,'gy'=4] {'gx','gy'}, use_global_device_ids=true, to_apply=%region_1.2 | all-reduce | flops 128 | bytes 1024 | tf_op jit(solution)/shard_map/psum | solution.py:97
  126.2 2.1 multiply_convert_fusion
  149.7 1.3 collective-permute-start.13
  151.0 4.6 %collective-permute-start.12 = (bf16[2,1,64,1,8,128]{5,2,4,3,1,0:T(8,128)(2,1)S(1)}, bf16[2,1,64,1,8,128]{5,2,4,3,1,0:T(8,128)(2,1)S(1)}, u32[]{:S(2)}, u32[]{:S(2)}) collective-permute-start(bf16[2,1,64,1,8,128]{5,2,4,3,1,0:T(8,128)(2,1)S(1)} %get-tuple-element.47), channel_id=1, source_target_pairs={{0,4},{4,8},{8,12},{1,5},{5,9},{9,13},{2,6},{6,10},{10,14},{3,7},{... | collective-permute-start | bytes 786440 | tf_op jit(solution)/shard_map/ppermute | solution.py:19
  163.9 1.3 collective-permute-start.15
  165.2 4.6 %collective-permute-start.14 = (bf16[2,1,64,4,1,128]{5,2,4,3,1,0:T(8,128)(2,1)S(1)}, bf16[2,1,64,4,1,128]{5,2,4,3,1,0:T(8,128)(2,1)S(1)}, u32[]{:S(2)}, u32[]{:S(2)}) collective-permute-start(bf16[2,1,64,4,1,128]{5,2,4,3,1,0:T(8,128)(2,1)S(1)} %get-tuple-element.41), channel_id=1, source_target_pairs={{0,1},{1,2},{2,3},{4,5},{5,6},{6,7},{8,9},{9,10},{10,11},{12,13},{... | collective-permute-start | bytes 393224 | tf_op jit(solution)/shard_map/ppermute | solution.py:19
  169.7 121.5 %all-reduce.7.cloned.1.call-done = f32[27,2048]{1,0:T(8,128)} async-done(((f32[27,2048]{1,0:T(8,128)}), f32[27,2048]{1,0:T(8,128)}) %all-reduce.7.cloned.1.call-update) | async-done | bytes 221200 | tf_op jit(solution)/shard_map/psum | solution.py:124
  291.3 1.7 multiply_reduce_fusion
  293.4 1.6 copy.591
  296.7 3.3 convolution_select_fusion
  300.0 1.8 copy.592
  303.9 2.4 broadcast_multiply_fusion
  306.3 2.7 fusion.39
  318.4 39.5 %all-reduce.3 = (f32[27,128]{1,0:T(8,128)S(1)}, f32[64,4]{0,1:T(4,128)S(1)}) all-reduce(f32[27,128]{1,0:T(8,128)S(1)} %stack.291, f32[64,4]{0,1:T(4,128)S(1)} %add_multiply_fusion), channel_id=1, replica_groups=mesh['dp'=2,'gx'=4,'gy'=4] {'dp','gx','gy'}, use_global_device_ids=true, to_apply=%region_4.5 | all-reduce | flops 3712 | bytes 29696 | tf_op jit(solution)/shard_map/psum | solution.py:124
  (400 shorter events, 64.5 us)
Async XLA Ops:
  7.2 117.2 %copy-start = (f32[64,4]{0,1:T(4,128)S(1)}, f32[64,4]{0,1:T(4,128)}, u32[]{:S(2)}) copy-start(f32[64,4]{0,1:T(4,128)} %param.17) | copy-start | bytes 3076
  7.2 21.5 %copy-start.13 = (f32[27,2048]{1,0:T(8,128)S(1)}, f32[27,2048]{1,0:T(8,128)}, u32[]{:S(2)}) copy-start(f32[27,2048]{1,0:T(8,128)} %param.20) | copy-start | bytes 663556
  7.2 284.1 %all-reduce.7.cloned.1.call-start = ((), (), s32[]{:S(2)}) async-start(), calls=%async_computation | async-start | bytes 524288 | tf_op jit(solution)/shard_map/psum | solution.py:124
  8.0 6.2 %collective-permute-start = (bf16[1,4,1,8,128]{4,1,3,2,0:T(4,128)(2,1)S(1)}, bf16[1,4,1,8,128]{4,1,3,2,0:T(4,128)(2,1)S(1)}, u32[]{:S(2)}, u32[]{:S(2)}) collective-permute-start(bf16[1,4,1,8,128]{4,1,3,2,0:T(4,128)(2,1)S(1)} %get-tuple-element.60), channel_id=1, source_target_pairs={{0,4},{4,8},{8,12},{1,5},{5,9},{9,13},{2,6},{6,10},{10,14},{3,7},{... | collective-permute-start | bytes 24584 | tf_op jit(solution)/shard_map/ppermute | solution.py:19
  12.9 5.5 %collective-permute-start.1 = (bf16[1,4,1,8,128]{4,1,3,2,0:T(4,128)(2,1)S(1)}, bf16[1,4,1,8,128]{4,1,3,2,0:T(4,128)(2,1)S(1)}, u32[]{:S(2)}, u32[]{:S(2)}) collective-permute-start(bf16[1,4,1,8,128]{4,1,3,2,0:T(4,128)(2,1)S(1)} %get-tuple-element.59), channel_id=1, source_target_pairs={{4,0},{8,4},{12,8},{5,1},{9,5},{13,9},{6,2},{10,6},{14,10},{7,3},{... | collective-permute-start | bytes 24584 | tf_op jit(solution)/shard_map/ppermute | solution.py:21
  14.2 15.8 %copy-start.46 = (bf16[1,4,1,8,128]{4,1,3,2,0:T(4,128)(2,1)}, bf16[1,4,1,8,128]{4,1,3,2,0:T(4,128)(2,1)S(1)}, u32[]{:S(2)}) copy-start(bf16[1,4,1,8,128]{4,1,3,2,0:T(4,128)(2,1)S(1)} %collective-permute-done) | copy-start | bytes 24580
  18.4 11.6 %copy-start.44 = (bf16[1,4,1,8,128]{4,1,3,2,0:T(4,128)(2,1)}, bf16[1,4,1,8,128]{4,1,3,2,0:T(4,128)(2,1)S(1)}, u32[]{:S(2)}) copy-start(bf16[1,4,1,8,128]{4,1,3,2,0:T(4,128)(2,1)S(1)} %collective-permute-done.1) | copy-start | bytes 24580
  18.4 42.6 %copy-start.28 = (bf16[1,4,4,8,128]{4,1,3,2,0:T(4,128)(2,1)}, bf16[1,4,4,8,128]{4,1,3,2,0:T(4,128)(2,1)S(1)}, u32[]{:S(2)}) copy-start(bf16[1,4,4,8,128]{4,1,3,2,0:T(4,128)(2,1)S(1)} %constant_dynamic-update-slice_fusion) | copy-start | bytes 98308
  18.5 11.4 %collective-permute-start.3 = (bf16[1,4,4,1,128]{4,1,3,2,0:T(4,128)(2,1)S(1)}, bf16[1,4,4,1,128]{4,1,3,2,0:T(4,128)(2,1)S(1)}, u32[]{:S(2)}, u32[]{:S(2)}) collective-permute-start(bf16[1,4,4,1,128]{4,1,3,2,0:T(4,128)(2,1)S(1)} %get-tuple-element.58), channel_id=1, source_target_pairs={{1,0},{2,1},{3,2},{5,4},{6,5},{7,6},{9,8},{10,9},{11,10},{13,12},{... | collective-permute-start | bytes 12296 | tf_op jit(solution)/shard_map/ppermute | solution.py:21
  19.8 10.1 %collective-permute-start.2 = (bf16[1,4,4,1,128]{4,1,3,2,0:T(4,128)(2,1)S(1)}, bf16[1,4,4,1,128]{4,1,3,2,0:T(4,128)(2,1)S(1)}, u32[]{:S(2)}, u32[]{:S(2)}) collective-permute-start(bf16[1,4,4,1,128]{4,1,3,2,0:T(4,128)(2,1)S(1)} %get-tuple-element.57), channel_id=1, source_target_pairs={{0,1},{1,2},{2,3},{4,5},{5,6},{6,7},{8,9},{9,10},{10,11},{12,13},{... | collective-permute-start | bytes 12296 | tf_op jit(solution)/shard_map/ppermute | solution.py:19
  29.9 31.2 %copy-start.42 = (bf16[1,4,4,1,128]{4,1,3,2,0:T(4,128)(2,1)}, bf16[1,4,4,1,128]{4,1,3,2,0:T(4,128)(2,1)S(1)}, u32[]{:S(2)}) copy-start(bf16[1,4,4,1,128]{4,1,3,2,0:T(4,128)(2,1)S(1)} %collective-permute-done.2) | copy-start | bytes 12292
  38.3 7.7 %copy-start.61 = (f32[2,8,8,17,32]{4,2,3,1,0:T(8,128)}, f32[2,8,8,17,32]{4,2,3,1,0:T(8,128)S(1)}, u32[]{:S(2)}) copy-start(f32[2,8,8,17,32]{4,2,3,1,0:T(8,128)S(1)} %fusion.38) | copy-start | bytes 835588
  46.5 14.6 %collective-permute-start.5 = (bf16[1,32,1,8,128]{4,1,3,2,0:T(8,128)(2,1)S(1)}, bf16[1,32,1,8,128]{4,1,3,2,0:T(8,128)(2,1)S(1)}, u32[]{:S(2)}, u32[]{:S(2)}) collective-permute-start(bf16[1,32,1,8,128]{4,1,3,2,0:T(8,128)(2,1)S(1)} %bitcast.753), channel_id=1, source_target_pairs={{4,0},{8,4},{12,8},{5,1},{9,5},{13,9},{6,2},{10,6},{14,10},{7,3},{... | collective-permute-start | bytes 196616 | tf_op jit(solution)/shard_map/ppermute | solution.py:21
  48.4 12.7 %collective-permute-start.4 = (bf16[1,32,1,8,128]{4,1,3,2,0:T(8,128)(2,1)S(1)}, bf16[1,32,1,8,128]{4,1,3,2,0:T(8,128)(2,1)S(1)}, u32[]{:S(2)}, u32[]{:S(2)}) collective-permute-start(bf16[1,32,1,8,128]{4,1,3,2,0:T(8,128)(2,1)S(1)} %bitcast.755), channel_id=1, source_target_pairs={{0,4},{4,8},{8,12},{1,5},{5,9},{9,13},{2,6},{6,10},{10,14},{3,7},{... | collective-permute-start | bytes 196616 | tf_op jit(solution)/shard_map/ppermute | solution.py:19
  53.6 13.4 %collective-permute-start.9 = (bf16[1,32,1,8,128]{4,1,3,2,0:T(8,128)(2,1)S(1)}, bf16[1,32,1,8,128]{4,1,3,2,0:T(8,128)(2,1)S(1)}, u32[]{:S(2)}, u32[]{:S(2)}) collective-permute-start(bf16[1,32,1,8,128]{4,1,3,2,0:T(8,128)(2,1)S(1)} %bitcast.754), channel_id=1, source_target_pairs={{4,0},{8,4},{12,8},{5,1},{9,5},{13,9},{6,2},{10,6},{14,10},{7,3},{... | collective-permute-start | bytes 196616 | tf_op jit(solution)/shard_map/ppermute | solution.py:21
  55.6 11.5 %collective-permute-start.8 = (bf16[1,32,1,8,128]{4,1,3,2,0:T(8,128)(2,1)S(1)}, bf16[1,32,1,8,128]{4,1,3,2,0:T(8,128)(2,1)S(1)}, u32[]{:S(2)}, u32[]{:S(2)}) collective-permute-start(bf16[1,32,1,8,128]{4,1,3,2,0:T(8,128)(2,1)S(1)} %bitcast.756), channel_id=1, source_target_pairs={{0,4},{4,8},{8,12},{1,5},{5,9},{9,13},{2,6},{6,10},{10,14},{3,7},{... | collective-permute-start | bytes 196616 | tf_op jit(solution)/shard_map/ppermute | solution.py:19
  61.1 12.5 %copy-start.3 = (bf16[1,32,1,8,128]{4,1,3,2,0:T(8,128)(2,1)}, bf16[1,32,1,8,128]{4,1,3,2,0:T(8,128)(2,1)S(1)}, u32[]{:S(2)}) copy-start(bf16[1,32,1,8,128]{4,1,3,2,0:T(8,128)(2,1)S(1)} %collective-permute-done.5) | copy-start | bytes 196612
  61.1 12.4 %copy-start.5 = (bf16[1,32,1,8,128]{4,1,3,2,0:T(8,128)(2,1)}, bf16[1,32,1,8,128]{4,1,3,2,0:T(8,128)(2,1)S(1)}, u32[]{:S(2)}) copy-start(bf16[1,32,1,8,128]{4,1,3,2,0:T(8,128)(2,1)S(1)} %collective-permute-done.4) | copy-start | bytes 196612
  61.2 12.4 %collective-permute-start.7 = (bf16[1,32,4,1,128]{4,1,3,2,0:T(8,128)(2,1)S(1)}, bf16[1,32,4,1,128]{4,1,3,2,0:T(8,128)(2,1)S(1)}, u32[]{:S(2)}, u32[]{:S(2)}) collective-permute-start(bf16[1,32,4,1,128]{4,1,3,2,0:T(8,128)(2,1)S(1)} %get-tuple-element.56), channel_id=1, source_target_pairs={{1,0},{2,1},{3,2},{5,4},{6,5},{7,6},{9,8},{10,9},{11,10},{13,12},{... | collective-permute-start | bytes 98312 | tf_op jit(solution)/shard_map/ppermute | solution.py:21
  62.5 11.1 %collective-permute-start.6 = (bf16[1,32,4,1,128]{4,1,3,2,0:T(8,128)(2,1)S(1)}, bf16[1,32,4,1,128]{4,1,3,2,0:T(8,128)(2,1)S(1)}, u32[]{:S(2)}, u32[]{:S(2)}) collective-permute-start(bf16[1,32,4,1,128]{4,1,3,2,0:T(8,128)(2,1)S(1)} %get-tuple-element.55), channel_id=1, source_target_pairs={{0,1},{1,2},{2,3},{4,5},{5,6},{6,7},{8,9},{9,10},{10,11},{12,13},{... | collective-permute-start | bytes 98312 | tf_op jit(solution)/shard_map/ppermute | solution.py:19
  67.1 9.0 %copy-start.10 = (bf16[1,32,1,8,128]{4,1,3,2,0:T(8,128)(2,1)}, bf16[1,32,1,8,128]{4,1,3,2,0:T(8,128)(2,1)S(1)}, u32[]{:S(2)}) copy-start(bf16[1,32,1,8,128]{4,1,3,2,0:T(8,128)(2,1)S(1)} %collective-permute-done.8) | copy-start | bytes 196612
  67.7 8.4 %collective-permute-start.11 = (bf16[1,32,4,1,128]{4,1,3,2,0:T(8,128)(2,1)}, bf16[1,32,4,1,128]{4,1,3,2,0:T(8,128)(2,1)S(1)}, u32[]{:S(2)}, u32[]{:S(2)}) collective-permute-start(bf16[1,32,4,1,128]{4,1,3,2,0:T(8,128)(2,1)} %get-tuple-element.54), channel_id=1, source_target_pairs={{1,0},{2,1},{3,2},{5,4},{6,5},{7,6},{9,8},{10,9},{11,10},{13,12},{... | collective-permute-start | bytes 98312 | tf_op jit(solution)/shard_map/ppermute | solution.py:21
  69.0 7.1 %collective-permute-start.10 = (bf16[1,32,4,1,128]{4,1,3,2,0:T(8,128)(2,1)}, bf16[1,32,4,1,128]{4,1,3,2,0:T(8,128)(2,1)S(1)}, u32[]{:S(2)}, u32[]{:S(2)}) collective-permute-start(bf16[1,32,4,1,128]{4,1,3,2,0:T(8,128)(2,1)} %get-tuple-element.53), channel_id=1, source_target_pairs={{0,1},{1,2},{2,3},{4,5},{5,6},{6,7},{8,9},{9,10},{10,11},{12,13},{... | collective-permute-start | bytes 98312 | tf_op jit(solution)/shard_map/ppermute | solution.py:19
  82.6 41.7 %copy-start.55 = (f32[1,4]{1,0:T(1,128)S(1)}, f32[1,4]{1,0:T(1,128)}, u32[]{:S(2)}) copy-start(f32[1,4]{1,0:T(1,128)} %param.12) | copy-start | bytes 52
  82.6 41.7 %copy-start.56 = (f32[4]{0:T(128)S(1)}, f32[4]{0:T(128)}, u32[]{:S(2)}) copy-start(f32[4]{0:T(128)} %param.18) | copy-start | bytes 52
  82.6 42.0 %copy-start.48 = (f32[64,4]{0,1:T(4,128)S(1)}, f32[64,4]{0,1:T(4,128)}, u32[]{:S(2)}) copy-start(f32[64,4]{0,1:T(4,128)} %param.21) | copy-start | bytes 3076
  149.7 14.2 %collective-permute-start.13 = (bf16[2,1,64,1,8,128]{5,2,4,3,1,0:T(8,128)(2,1)S(1)}, bf16[2,1,64,1,8,128]{5,2,4,3,1,0:T(8,128)(2,1)S(1)}, u32[]{:S(2)}, u32[]{:S(2)}) collective-permute-start(bf16[2,1,64,1,8,128]{5,2,4,3,1,0:T(8,128)(2,1)S(1)} %get-tuple-element.48), channel_id=1, source_target_pairs={{4,0},{8,4},{12,8},{5,1},{9,5},{13,9},{6,2},{10,6},{14,10},{7,3},{... | collective-permute-start | bytes 786440 | tf_op jit(solution)/shard_map/ppermute | solution.py:21
  151.0 12.9 %collective-permute-start.12 = (bf16[2,1,64,1,8,128]{5,2,4,3,1,0:T(8,128)(2,1)S(1)}, bf16[2,1,64,1,8,128]{5,2,4,3,1,0:T(8,128)(2,1)S(1)}, u32[]{:S(2)}, u32[]{:S(2)}) collective-permute-start(bf16[2,1,64,1,8,128]{5,2,4,3,1,0:T(8,128)(2,1)S(1)} %get-tuple-element.47), channel_id=1, source_target_pairs={{0,4},{4,8},{8,12},{1,5},{5,9},{9,13},{2,6},{6,10},{10,14},{3,7},{... | collective-permute-start | bytes 786440 | tf_op jit(solution)/shard_map/ppermute | solution.py:19
  162.9 128.3 %copy-start.14 = (f32[27,2048]{1,0:T(8,128)S(1)}, f32[27,2048]{1,0:T(8,128)}, u32[]{:S(2)}) copy-start(f32[27,2048]{1,0:T(8,128)} %param.20) | copy-start | bytes 663556
  163.9 129.1 %collective-permute-start.15 = (bf16[2,1,64,4,1,128]{5,2,4,3,1,0:T(8,128)(2,1)S(1)}, bf16[2,1,64,4,1,128]{5,2,4,3,1,0:T(8,128)(2,1)S(1)}, u32[]{:S(2)}, u32[]{:S(2)}) collective-permute-start(bf16[2,1,64,4,1,128]{5,2,4,3,1,0:T(8,128)(2,1)S(1)} %get-tuple-element.42), channel_id=1, source_target_pairs={{1,0},{2,1},{3,2},{5,4},{6,5},{7,6},{9,8},{10,9},{11,10},{13,12},{... | collective-permute-start | bytes 393224 | tf_op jit(solution)/shard_map/ppermute | solution.py:21
  165.2 127.8 %collective-permute-start.14 = (bf16[2,1,64,4,1,128]{5,2,4,3,1,0:T(8,128)(2,1)S(1)}, bf16[2,1,64,4,1,128]{5,2,4,3,1,0:T(8,128)(2,1)S(1)}, u32[]{:S(2)}, u32[]{:S(2)}) collective-permute-start(bf16[2,1,64,4,1,128]{5,2,4,3,1,0:T(8,128)(2,1)S(1)} %get-tuple-element.41), channel_id=1, source_target_pairs={{0,1},{1,2},{2,3},{4,5},{5,6},{6,7},{8,9},{9,10},{10,11},{12,13},{... | collective-permute-start | bytes 393224 | tf_op jit(solution)/shard_map/ppermute | solution.py:19
  314.0 43.8 %copy-start.32 = (f32[27,128]{1,0:T(8,128)S(1)}, f32[27,128]{1,0:T(8,128)}, u32[]{:S(2)}) copy-start(f32[27,128]{1,0:T(8,128)} %param.19) | copy-start | bytes 41476
  (49 other events, 109.7 us)
Sparse Core Ops, SparseCore 0:
  163.8 127.3 all-reduce.6
where the time goes:
time: 380 us; the launch traced here: 376 us
  waiting for transfers between devices  125 us (33%)
  blocking collectives  78.7 us (21%)
  matrix products  54.8 us (14%)
  starting transfers between devices  48.4 us (13%)
  local copies, waits for them, and re-layouts  35.4 us (9%)
  between operations  23.2 us (6%)
  other arithmetic  10.9 us (3%)
    psum x1, waiting for transfers between devices, per_device(): h1, h2, hd = lax.psum((h1, h2, hd), ('dp', 'gx', 'gy'))  122 us
    psum x1, blocking collectives, per_device(): h1, h2, hd = lax.psum((h1, h2, hd), ('dp', 'gx', 'gy'))  39.5 us
    psum x1, blocking collectives, per_device(): lax.psum((jnp.sum(act2, axis=(2, 3, 4)), jnp.sum(slope2 * t2, axis=(2, 3,...  39.3 us
    ppermute x8, starting transfers between devices, extended(): lax.ppermute(tail, axis, [(i, (i + 1) % count) for i in range(ends)])  38 us
    conv_general_dilated x8, matrix products, convolve(): lax.conv_general_dilated(pad_depth(padded), kernel, (1, 1, 1), 'VALID', d...  28.8 us
    dot_general x81, matrix products, correlate(): jnp.einsum('bixyz,boxyz->oi', window, grads, preferred_element_type=jnp.f...  25.3 us
    unnamed x145, local copies, waits for them, and re-layouts  13.8 us
    ppermute x8, starting transfers between devices, extended(): lax.ppermute(head, axis, [((i + 1) % count, i) for i in range(ends)])  10.3 us
  transfers between devices with their start and end apart: 17, of which 2 were waited for; matrix products, arithmetic and copies ran while one was open for 5% of the time, Pallas kernels for 0%

commit v1 on v0

v1 whole, which is shorter than its diff:
```python
import jax
import jax.numpy as jnp
from jax import lax
from jax.experimental import pallas as pl
from jax.experimental.pallas import tpu as pltpu
from jax.sharding import PartitionSpec as P

C0 = 4
C1 = 32
C2 = 64
ROWS = 16
F32 = jnp.float32
BF16 = jnp.bfloat16


def extended(cells, sides, width):
    for axis, dim in sides:
        count = lax.axis_size(axis)
        ends = count - 1
        head = lax.slice_in_dim(cells, 0, width, axis=dim)
        tail = lax.slice_in_dim(cells, cells.shape[dim] - width, cells.shape[dim], axis=dim)
        cells = jnp.concatenate(
            [
                lax.ppermute(tail, axis, [(i, (i + 1) % count) for i in range(ends)]),
                cells,
                lax.ppermute(head, axis, [((i + 1) % count, i) for i in range(ends)]),
            ],
            axis=dim,
        )
    return cells


def silu_parts(z):
    s = 1.0 / (1.0 + jnp.exp(-z))
    return (z * s, s * (1.0 + z * (1.0 - s)), s * (1.0 - s) * (2.0 + z * (1.0 - 2.0 * s)))


def window(ref, x, y, count):
    columns = []
    for k in range(count):
        parts = []
        for a in range(3):
            rows = ref[x + a, y + k : y + k + 3]
            parts.append(rows.reshape(rows.shape[0] * rows.shape[1], rows.shape[2]))
        columns.append(jnp.concatenate(parts, axis=0))
    return jnp.concatenate(columns, axis=1)


def lane_of(shape):
    return lax.broadcasted_iota(jnp.int32, shape, 1)


def from_left(u):
    return jnp.where(lane_of(u.shape) == 0, 0.0, pltpu.roll(u, 1, 1))


def from_right(u):
    last = u.shape[1] - 1
    return jnp.where(lane_of(u.shape) == last, 0.0, pltpu.roll(u, last, 1))


def gathered(y, n):
    return from_left(y[:n]) + y[n : 2 * n] + from_right(y[2 * n : 3 * n])


def forward_kernel(v_ref, l1_ref, b1_ref, l2_ref, b2_ref, pq_ref, a_ref, ta_ref, d_ref, pool_ref, tpool_ref):
    nx, ny, lanes = (pq_ref.shape[1], pq_ref.shape[2], pq_ref.shape[4])
    b1 = b1_ref[...]
    l1 = l1_ref[...]
    for x in range(nx + 2):
        for y in range(0, ny + 2, 2):
            res = jnp.dot(l1, window(v_ref, x, y, 2), preferred_element_type=F32)
            for k in range(2):
                part = res[:, k * lanes : (k + 1) * lanes]
                z1 = part[:C1] + b1
                t1 = part[C1:]
                mask = v_ref[x + 1, y + k + 1].astype(F32)[3 * C0 : 3 * C0 + 1]
                act, slope, bend = silu_parts(z1)
                a_ref[x, y + k] = (act * mask).astype(BF16)
                ta_ref[x, y + k] = (slope * t1 * mask).astype(BF16)
                if 1 <= x <= nx and 1 <= y + k <= ny:
                    d_ref[0, x - 1, y + k - 1] = slope.astype(BF16)
                    d_ref[1, x - 1, y + k - 1] = (bend * t1).astype(BF16)
    b2 = b2_ref[...]
    n = 3 * C2
    total = jnp.zeros((C2, lanes), F32)
    ttotal = jnp.zeros((C2, lanes), F32)
    for x in range(nx):
        for y in range(0, ny, 2):
            res = jnp.dot(l2_ref[...], window(a_ref, x, y, 2), preferred_element_type=F32)
            tres = res[n:] + jnp.dot(l2_ref[:n], window(ta_ref, x, y, 2), preferred_element_type=F32)
            for k in range(2):
                z2 = gathered(res[:n, k * lanes : (k + 1) * lanes], C2) + b2
                t2 = gathered(tres[:, k * lanes : (k + 1) * lanes], C2)
                act, slope, bend = silu_parts(z2)
                total = total + act
                ttotal = ttotal + slope * t2
                pq_ref[0, x, y + k] = slope.astype(BF16)
                pq_ref[1, x, y + k] = (bend * t2).astype(BF16)
    pool_ref[...] = jnp.sum(total, axis=1, keepdims=True)
    tpool_ref[...] = jnp.sum(ttotal, axis=1, keepdims=True)


NT = (((1,), (1,)), ((), ()))


def backward_kernel(
    cells, batch, pq_ref, a_ref, ta_ref, d_ref, v_ref, lb_ref, pool_ref, tpool_ref, targets_ref,
    head_w_ref, head_b_ref, dir_head_ref, h2_ref, h1_ref, hd_ref, field_ref, g_ref, tg_ref, t1_ref,
):
    nx, ny, lanes = (d_ref.shape[1], d_ref.shape[2], d_ref.shape[4])
    pooled = pool_ref[...] / cells
    tpooled = tpool_ref[...] / cells
    head_w = head_w_ref[...]
    dir_head = dir_head_ref[...]
    out = jnp.sum(pooled * head_w, axis=0, keepdims=True) + head_b_ref[...]
    tout = jnp.sum(tpooled * head_w + pooled * dir_head, axis=0, keepdims=True)
    dy = (out - targets_ref[...]) / batch
    tdy = tout / batch
    hd_ref[...] = tpooled * dy + pooled * tdy
    dpool = jnp.sum(dy * head_w, axis=1, keepdims=True) / cells
    tdpool = jnp.sum(tdy * head_w + dy * dir_head, axis=1, keepdims=True) / cells
    for x in range(nx + 2):
        for y in range(ny + 2):
            slope = pq_ref[0, x, y].astype(F32)
            bent = pq_ref[1, x, y].astype(F32)
            g_ref[x, y] = (slope * dpool).astype(BF16)
            tg_ref[x, y] = (bent * dpool + slope * tdpool).astype(BF16)

    def moved(ref, x, y):
        columns = []
        for k in range(2):
            u = ref[x + 1, y + k + 1].astype(F32)
            columns.append(jnp.concatenate([from_right(u), u, from_left(u)], axis=0).astype(BF16))
        return jnp.concatenate(columns, axis=1)

    h2 = jnp.zeros(h2_ref.shape, F32)
    for x in range(nx):
        for y in range(0, ny, 2):
            h2 = h2 + lax.dot_general(moved(tg_ref, x, y), window(a_ref, x, y, 2), NT, preferred_element_type=F32)
            h2 = h2 + lax.dot_general(moved(g_ref, x, y), window(ta_ref, x, y, 2), NT, preferred_element_type=F32)
    h2_ref[...] = h2
    n = 3 * C1
    h1 = jnp.zeros(h1_ref.shape, F32)
    for x in range(nx):
        for y in range(0, ny, 2):
            res = jnp.dot(lb_ref[...], window(g_ref, x, y, 2), preferred_element_type=F32)
            tres = res[n:] + jnp.dot(lb_ref[:n], window(tg_ref, x, y, 2), preferred_element_type=F32)
            grads = []
            for k in range(2):
                da = gathered(res[:n, k * lanes : (k + 1) * lanes], C1)
                tda = gathered(tres[:, k * lanes : (k + 1) * lanes], C1)
                field_ref[:, x, y + k, :] = tda * cells
                grads.append((d_ref[1, x, y + k].astype(F32) * da + d_ref[0, x, y + k].astype(F32) * tda).astype(BF16))
            h1 = h1 + lax.dot_general(
                jnp.concatenate(grads, axis=1), window(v_ref, x + 1, y + 1, 2), NT, preferred_element_type=F32
            )
    h1_ref[...] = h1


def vmem_call(kernel, shapes, scratch=()):
    return pl.pallas_call(
        kernel,
        out_shape=shapes,
        scratch_shapes=scratch,
        compiler_params=pltpu.CompilerParams(vmem_limit_bytes=48 * 1024 * 1024),
    )


def per_device(
    volume, targets, conv1_w, conv1_b, conv2_w, conv2_b, head_w, head_b, dir1, dir2, dir_head
):
    nx, ny, lanes = volume.shape[2:]
    cells = nx * lax.axis_size("gx") * ny * lax.axis_size("gy") * lanes
    batch = volume.shape[0] * lax.axis_size("dp")
    rows = volume[0].transpose(1, 2, 0, 3)
    wide = jnp.pad(rows, ((0, 0), (0, 0), (0, 0), (1, 1)))
    v = jnp.concatenate(
        [wide[..., :lanes], rows, wide[..., 2:], jnp.ones((nx, ny, 1, lanes), BF16), jnp.zeros((nx, ny, 3, lanes), BF16)],
        axis=2,
    )
    v = extended(v, (("gx", 0), ("gy", 1)), 2)
    first = jnp.stack((conv1_w, dir1.astype(BF16))).reshape(2, 9, 3, C1, C0)
    first = first.transpose(0, 3, 1, 2, 4).reshape(2 * C1, 9, 3 * C0)
    l1 = jnp.pad(first, ((0, 0), (0, 0), (0, ROWS - 3 * C0))).reshape(2 * C1, 9 * ROWS)
    second = jnp.stack((conv2_w, dir2.astype(BF16))).reshape(2, 9, 3, C2, C1)
    l2 = second.transpose(0, 2, 3, 1, 4).reshape(6 * C2, 9 * C1)
    lb = jnp.flip(second, (1, 2)).transpose(0, 2, 4, 1, 3).reshape(6 * C1, 9 * C2)
    shape = jax.ShapeDtypeStruct
    pq, a1, ta1, d, pool, tpool = vmem_call(
        forward_kernel,
        (
            shape((2, nx, ny, C2, lanes), BF16),
            shape((nx + 2, ny + 2, C1, lanes), BF16),
            shape((nx + 2, ny + 2, C1, lanes), BF16),
            shape((2, nx, ny, C1, lanes), BF16),
            shape((C2, 1), F32),
            shape((C2, 1), F32),
        ),
    )(v, l1, conv1_b[:, None], l2, conv2_b[:, None])
    pool, tpool = lax.psum((pool, tpool), ("gx", "gy"))
    pq = extended(pq, (("gx", 1), ("gy", 2)), 1)

    def backward(*refs):
        backward_kernel(cells, batch, *refs)

    h2, h1, hd, field = vmem_call(
        backward,
        (
            shape((3 * C2, 9 * C1), F32),
            shape((C1, 9 * ROWS), F32),
            shape((C2, head_w.shape[1]), F32),
            shape((C1, nx, ny, lanes), F32),
        ),
        (
            pltpu.VMEM((nx + 2, ny + 2, C2, lanes), BF16),
            pltpu.VMEM((nx + 2, ny + 2, C2, lanes), BF16),
            pltpu.VMEM((8, lanes), F32),
        ),
    )(pq, a1, ta1, d, v, lb, pool, tpool, targets, head_w, head_b[None], dir_head)
    leader = ((lax.axis_index("gx") == 0) & (lax.axis_index("gy") == 0)).astype(F32)
    h2, h1, hd = lax.psum((h2, h1, leader * hd), ("dp", "gx", "gy"))
    h2 = h2.reshape(3, C2, 9, C1).transpose(2, 0, 1, 3).reshape(27, C2 * C1)
    h1 = h1.reshape(C1, 9, ROWS)[:, :, : 3 * C0].reshape(C1, 27, C0).transpose(1, 0, 2).reshape(27, C1 * C0)
    quad = jnp.sum(dir1 * h1) + jnp.sum(dir2 * h2) + jnp.sum(dir_head * hd)
    length = jnp.sum(dir1 * dir1) + jnp.sum(dir2 * dir2) + jnp.sum(dir_head * dir_head)
    nrm = jnp.sqrt(jnp.sum(h1 * h1) + jnp.sum(h2 * h2) + jnp.sum(hd * hd) + 1e-06)
    return (h1 / nrm, h2 / nrm, hd / nrm, quad / length, field[None])


def solution(mesh):
    return jax.shard_map(
        per_device,
        mesh=mesh,
        in_specs=(P("dp", None, "gx", "gy", None), P("dp", None)) + (P(),) * 9,
        out_specs=(P(), P(), P(), P(), P("dp", None, "gx", "gy", None)),
        check_vma=False,
    )
```

time: 380 us -> 329 us (0.87)
  matrix products: 54.8 us -> 0 us
  blocking collectives: 78.7 us -> 113 us
  starting transfers between devices: 48.4 us -> 22.5 us
  local copies, waits for them, and re-layouts: 35.4 us -> 14.2 us
  waiting for transfers between devices: 125 us -> 142 us
  Pallas kernels: 0 us -> 6.25 us
    psum x2, blocking collectives: 78.7 us -> 113 us  [the longest x1 74.8 us: per_device(): pool, tpool = lax.psum((pool, tpool), ('gx', 'gy'))]
    conv_general_dilated x8 -> x0, matrix products: 28.8 us -> none  [convolve(): lax.conv_general_dilated(pad_depth(padded), kernel, (1, 1, 1), 'VALID', d...]
    dot_general x87 -> x0, matrix products: 26.1 us -> none  [the longest x81 25.3 us: correlate(): jnp.einsum('bixyz,boxyz->oi', window, grads, preferred_element_type=jnp.f...]
    ppermute x8 -> x4, starting transfers between devices: 38 us -> 17.3 us  [extended(): lax.ppermute(tail, axis, [(i, (i + 1) % count) for i in range(ends)])]
    unnamed x145 -> x33, local copies, waits for them, and re-layouts: 13.8 us -> 3.21 us
    psum x1, waiting for transfers between devices: 122 us -> 130 us  [per_device(): h2, h1, hd = lax.psum((h2, h1, leader * hd), ('dp', 'gx', 'gy'))]
    another operation x84 -> x7, local copies, waits for them, and re-layouts: 9.29 us -> 2.84 us  [the longest x4 2.15 us: per_device(): first = jnp.stack((conv1_w, dir1.astype(BF16))).reshape(2, 9, 3, C1, C0)]
    pallas_call x0 -> x2, Pallas kernels: none -> 6.25 us  [the longest x1 4.26 us: per_device(): vmem_call(backward, (shape((3 * C2, 9 * C1), F32), shape((C1, 9 * ROWS),...]
  transfers between devices with their start and end apart: 17 -> 9, of which waited for: 2 -> 4; matrix products, arithmetic and copies ran while one was open for 5% -> 4% of each run, Pallas kernels for 0% -> 0%
where the time goes in v1:
time: 329 us; the launch traced here: 328 us
  waiting for transfers between devices  142 us (43%)
  blocking collectives  113 us (34%)
  starting transfers between devices  22.5 us (7%)
  between operations  21.4 us (7%)
  local copies, waits for them, and re-layouts  14.2 us (4%)
  other arithmetic  8.64 us (3%)
  Pallas kernels  6.25 us (2%)
    psum x1, waiting for transfers between devices, per_device(): h2, h1, hd = lax.psum((h2, h1, leader * hd), ('dp', 'gx', 'gy'))  130 us
    psum x1, blocking collectives, per_device(): pool, tpool = lax.psum((pool, tpool), ('gx', 'gy'))  74.8 us
    psum x1, blocking collectives, per_device(): h2, h1, hd = lax.psum((h2, h1, leader * hd), ('dp', 'gx', 'gy'))  38.5 us
    ppermute x4, starting transfers between devices, extended(): lax.ppermute(tail, axis, [(i, (i + 1) % count) for i in range(ends)])  17.3 us
    ppermute x4, waiting for transfers between devices, extended(): lax.ppermute(head, axis, [((i + 1) % count, i) for i in range(ends)])  9.28 us
  transfers between devices with their start and end apart: 9, of which 4 were waited for; matrix products, arithmetic and copies ran while one was open for 4% of the time, Pallas kernels for 0%

profile of v1, /device:TPU:0, one launch (start us, length us, event | category | flops | bytes accessed | tf_op | source)
XLA Modules:
  0.0 327.9 jit_solution(15966052681875612160)
XLA Ops:
  7.2 0.8 copy.68
  8.2 1.3 collective-permute-start.1
  9.5 5.5 %collective-permute-start = (bf16[2,8,16,128]{3,2,1,0:T(8,128)(2,1)S(1)}, bf16[2,8,16,128]{3,2,1,0:T(8,128)(2,1)S(1)}, u32[]{:S(2)}, u32[]{:S(2)}) collective-permute-start(bf16[2,8,16,128]{3,2,1,0:T(8,128)(2,1)S(1)} %concatenate.17), channel_id=1, source_target_pairs={{0,4},{4,8},{8,12},{1,5},{5,9},{9,13},{2,6},{6,10},{10,14},{3,7},{... | collective-permute-start | bytes 196616 | tf_op jit(solution)/shard_map/ppermute | solution.py:24
  15.0 1.4 multiply_reduce_fusion.7
  16.4 1.0 convert_element_type.14
  18.1 1.2 stack.18
  20.4 4.0 %collective-permute-start.2 = (bf16[6,2,16,128]{3,2,1,0:T(8,128)(2,1)S(1)}, bf16[6,2,16,128]{3,2,1,0:T(8,128)(2,1)S(1)}, u32[]{:S(2)}, u32[]{:S(2)}) collective-permute-start(bf16[6,2,16,128]{3,2,1,0:T(8,128)(2,1)S(1)} %get-tuple-element.53), channel_id=1, source_target_pairs={{0,1},{1,2},{2,3},{4,5},{5,6},{6,7},{8,9},{9,10},{10,11},{12,13},{... | collective-permute-start | bytes 147464 | tf_op jit(solution)/shard_map/ppermute | solution.py:24
  24.4 1.3 collective-permute-start.3
  26.2 0.7 copy.51
  27.6 2.8 collective-permute-done.3
  30.4 2.0 shard_map.146
  32.5 4.3 %collective-permute-start.4 = (bf16[2,1,8,64,128]{4,3,2,1,0:T(8,128)(2,1)S(1)}, bf16[2,1,8,64,128]{4,3,2,1,0:T(8,128)(2,1)S(1)}, u32[]{:S(2)}, u32[]{:S(2)}) collective-permute-start(bf16[2,1,8,64,128]{4,3,2,1,0:T(8,128)(2,1)S(1)} %get-tuple-element.51), channel_id=1, source_target_pairs={{0,4},{4,8},{8,12},{1,5},{5,9},{9,13},{2,6},{6,10},{10,14},{3,7},{... | collective-permute-start | bytes 786440 | tf_op jit(solution)/shard_map/ppermute | solution.py:24
  36.8 1.3 collective-permute-start.5
  38.1 2.6 collective-permute-done.4
  40.7 6.5 %collective-permute-done.5 = bf16[2,1,8,64,128]{4,3,2,1,0:T(8,128)(2,1)S(1)} collective-permute-done((bf16[2,1,8,64,128]{4,3,2,1,0:T(8,128)(2,1)S(1)}, bf16[2,1,8,64,128]{4,3,2,1,0:T(8,128)(2,1)S(1)}, u32[]{:S(2)}, u32[]{:S(2)}) %collective-permute-start.5) | collective-permute-done | bytes 262176 | tf_op jit(solution)/shard_map/ppermute | solution.py:26
  47.3 0.7 fusion
  48.0 3.5 %collective-permute-start.6 = (bf16[2,4,1,64,128]{4,3,2,1,0:T(8,128)(2,1)}, bf16[2,4,1,64,128]{4,3,2,1,0:T(8,128)(2,1)S(1)}, u32[]{:S(2)}, u32[]{:S(2)}) collective-permute-start(bf16[2,4,1,64,128]{4,3,2,1,0:T(8,128)(2,1)} %get-tuple-element.48), channel_id=1, source_target_pairs={{0,1},{1,2},{2,3},{4,5},{5,6},{6,7},{8,9},{9,10},{10,11},{12,13},{... | collective-permute-start | bytes 393224 | tf_op jit(solution)/shard_map/ppermute | solution.py:24
  51.5 1.3 collective-permute-start.7
  53.2 1.5 copy.56
  54.8 1.6 reshape.50.refs_5_
  56.4 0.7 multiply_reduce_fusion.8
  57.0 74.8 %all-reduce.3 = (f32[64,1]{1,0:T(8,128)S(1)}, f32[64,1]{1,0:T(8,128)S(1)}) all-reduce(f32[64,1]{1,0:T(8,128)S(1)} %get-tuple-element.19, f32[64,1]{1,0:T(8,128)S(1)} %get-tuple-element.20), channel_id=1, replica_groups=mesh['dp'=2,'gx'=4,'gy'=4] {'gx','gy'}, use_global_device_ids=true, to_apply=%region_0.1 | all-reduce | flops 128 | bytes 1024 | tf_op jit(solution)/shard_map/psum | solution.py:201
  132.5 4.3 %shard_map.147 = (f32[192,288]{1,0:T(8,128)S(1)}, f32[32,144]{1,0:T(8,128)S(1)}, f32[64,4]{1,0:T(8,128)S(1)}, f32[32,2,8,128]{3,2,1,0:T(8,128)}) custom-call(bf16[2,4,10,64,128]{4,3,2,1,0:T(8,128)(2,1)S(1)} %pad_maximum_fusion.refs_0_, bf16[4,10,32,128]{3,2,1,0:T(8,128)(2,1)S(1)} %get-tuple-element.16.refs_1_, ...), custom_call_target="tpu_custom_call" | custom-call | tf_op jit(solution)/shard_map/pallas_call | solution.py:207
  136.9 38.5 %all-reduce.2 = (f32[32,9,16]{0,2,1:T(8,128)S(1)}, f32[64,4]{1,0:T(8,128)S(1)}) all-reduce(f32[32,9,16]{0,2,1:T(8,128)S(1)} %bitcast.35, f32[64,4]{1,0:T(8,128)S(1)} %broadcast_multiply_fusion), channel_id=1, replica_groups=mesh['dp'=2,'gx'=4,'gy'=4] {'dp','gx','gy'}, use_global_device_ids=true, to_apply=%region_2.3 | all-reduce | flops 4864 | bytes 38912 | tf_op jit(solution)/shard_map/psum | solution.py:222
  175.3 0.6 multiply_reduce_fusion.4
  176.2 1.0 reshape.54
  177.3 0.6 multiply_reduce_fusion.5
  177.9 129.8 %all-reduce.6.cloned.1.call-done = f32[9,3,64,32]{2,1,3,0:T(4,128)} async-done(((f32[9,3,64,32]{2,1,3,0:T(4,128)}), f32[9,3,64,32]{2,1,3,0:T(4,128)}) %all-reduce.6.cloned.1.call-update) | async-done | bytes 221200 | tf_op jit(solution)/shard_map/psum | solution.py:222
  307.7 2.0 multiply_reduce_fusion
  312.4 0.7 copy.65
  313.1 0.7 copy.66
  314.7 1.4 multiply_reduce_fusion.1
  (71 shorter events, 6.3 us)
Async XLA Ops:
  7.2 12.7 %copy-start.6 = (bf16[27,2048]{1,0:T(8,128)(2,1)S(1)}, bf16[27,2048]{1,0:T(8,128)(2,1)}, u32[]{:S(2)}) copy-start(bf16[27,2048]{1,0:T(8,128)(2,1)} %param.15) | copy-start | bytes 331780
  7.2 300.6 %all-reduce.6.cloned.1.call-start = ((), (), s32[]{:S(2)}) async-start(), calls=%async_computation | async-start | bytes 1179648 | tf_op jit(solution)/shard_map/psum | solution.py:222
  8.2 12.1 %collective-permute-start.1 = (bf16[2,8,16,128]{3,2,1,0:T(8,128)(2,1)S(1)}, bf16[2,8,16,128]{3,2,1,0:T(8,128)(2,1)S(1)}, u32[]{:S(2)}, u32[]{:S(2)}) collective-permute-start(bf16[2,8,16,128]{3,2,1,0:T(8,128)(2,1)S(1)} %concatenate.17), channel_id=1, source_target_pairs={{4,0},{8,4},{12,8},{5,1},{9,5},{13,9},{6,2},{10,6},{14,10},{7,3},{... | collective-permute-start | bytes 196616 | tf_op jit(solution)/shard_map/ppermute | solution.py:26
  9.5 10.9 %collective-permute-start = (bf16[2,8,16,128]{3,2,1,0:T(8,128)(2,1)S(1)}, bf16[2,8,16,128]{3,2,1,0:T(8,128)(2,1)S(1)}, u32[]{:S(2)}, u32[]{:S(2)}) collective-permute-start(bf16[2,8,16,128]{3,2,1,0:T(8,128)(2,1)S(1)} %concatenate.17), channel_id=1, source_target_pairs={{0,4},{4,8},{8,12},{1,5},{5,9},{9,13},{2,6},{6,10},{10,14},{3,7},{... | collective-permute-start | bytes 196616 | tf_op jit(solution)/shard_map/ppermute | solution.py:24
  19.9 5.9 %copy-start.11 = (f32[32]{0:T(128)S(1)}, f32[32]{0:T(128)}, u32[]{:S(2)}) copy-start(f32[32]{0:T(128)} %param.14) | copy-start | bytes 388
  19.9 6.0 %copy-start.10 = (f32[64]{0:T(128)S(1)}, f32[64]{0:T(128)}, u32[]{:S(2)}) copy-start(f32[64]{0:T(128)} %param.16) | copy-start | bytes 772
  20.4 7.2 %collective-permute-start.2 = (bf16[6,2,16,128]{3,2,1,0:T(8,128)(2,1)S(1)}, bf16[6,2,16,128]{3,2,1,0:T(8,128)(2,1)S(1)}, u32[]{:S(2)}, u32[]{:S(2)}) collective-permute-start(bf16[6,2,16,128]{3,2,1,0:T(8,128)(2,1)S(1)} %get-tuple-element.53), channel_id=1, source_target_pairs={{0,1},{1,2},{2,3},{4,5},{5,6},{6,7},{8,9},{9,10},{10,11},{12,13},{... | collective-permute-start | bytes 147464 | tf_op jit(solution)/shard_map/ppermute | solution.py:24
  24.4 6.0 %collective-permute-start.3 = (bf16[6,2,16,128]{3,2,1,0:T(8,128)(2,1)S(1)}, bf16[6,2,16,128]{3,2,1,0:T(8,128)(2,1)S(1)}, u32[]{:S(2)}, u32[]{:S(2)}) collective-permute-start(bf16[6,2,16,128]{3,2,1,0:T(8,128)(2,1)S(1)} %get-tuple-element.54), channel_id=1, source_target_pairs={{1,0},{2,1},{3,2},{5,4},{6,5},{7,6},{9,8},{10,9},{11,10},{13,12},{... | collective-permute-start | bytes 147464 | tf_op jit(solution)/shard_map/ppermute | solution.py:26
  32.5 8.2 %collective-permute-start.4 = (bf16[2,1,8,64,128]{4,3,2,1,0:T(8,128)(2,1)S(1)}, bf16[2,1,8,64,128]{4,3,2,1,0:T(8,128)(2,1)S(1)}, u32[]{:S(2)}, u32[]{:S(2)}) collective-permute-start(bf16[2,1,8,64,128]{4,3,2,1,0:T(8,128)(2,1)S(1)} %get-tuple-element.51), channel_id=1, source_target_pairs={{0,4},{4,8},{8,12},{1,5},{5,9},{9,13},{2,6},{6,10},{10,14},{3,7},{... | collective-permute-start | bytes 786440 | tf_op jit(solution)/shard_map/ppermute | solution.py:24
  36.8 10.5 %collective-permute-start.5 = (bf16[2,1,8,64,128]{4,3,2,1,0:T(8,128)(2,1)S(1)}, bf16[2,1,8,64,128]{4,3,2,1,0:T(8,128)(2,1)S(1)}, u32[]{:S(2)}, u32[]{:S(2)}) collective-permute-start(bf16[2,1,8,64,128]{4,3,2,1,0:T(8,128)(2,1)S(1)} %get-tuple-element.50), channel_id=1, source_target_pairs={{4,0},{8,4},{12,8},{5,1},{9,5},{13,9},{6,2},{10,6},{14,10},{7,3},{... | collective-permute-start | bytes 786440 | tf_op jit(solution)/shard_map/ppermute | solution.py:26
  40.7 12.2 %copy-start.7 = (f32[27,128]{1,0:T(8,128)S(1)}, f32[27,128]{1,0:T(8,128)}, u32[]{:S(2)}) copy-start(f32[27,128]{1,0:T(8,128)} %param.19) | copy-start | bytes 41476
  47.3 5.6 %copy-start.2 = (bf16[2,4,8,64,128]{4,3,2,1,0:T(8,128)(2,1)}, bf16[2,4,8,64,128]{4,3,2,1,0:T(8,128)(2,1)S(1)}, u32[]{:S(2)}) copy-start(bf16[2,4,8,64,128]{4,3,2,1,0:T(8,128)(2,1)S(1)} %constant_dynamic-update-slice_fusion.2) | copy-start | bytes 3145732
  47.3 5.7 %copy-start.8 = (f32[64,4]{0,1:T(4,128)S(1)}, f32[64,4]{0,1:T(4,128)}, u32[]{:S(2)}) copy-start(f32[64,4]{0,1:T(4,128)} %param.21) | copy-start | bytes 3076
  47.3 5.8 %copy-start.9 = (f32[64,4]{0,1:T(4,128)S(1)}, f32[64,4]{0,1:T(4,128)}, u32[]{:S(2)}) copy-start(f32[64,4]{0,1:T(4,128)} %param.17) | copy-start | bytes 3076
  48.0 83.8 %collective-permute-start.6 = (bf16[2,4,1,64,128]{4,3,2,1,0:T(8,128)(2,1)}, bf16[2,4,1,64,128]{4,3,2,1,0:T(8,128)(2,1)S(1)}, u32[]{:S(2)}, u32[]{:S(2)}) collective-permute-start(bf16[2,4,1,64,128]{4,3,2,1,0:T(8,128)(2,1)} %get-tuple-element.48), channel_id=1, source_target_pairs={{0,1},{1,2},{2,3},{4,5},{5,6},{6,7},{8,9},{9,10},{10,11},{12,13},{... | collective-permute-start | bytes 393224 | tf_op jit(solution)/shard_map/ppermute | solution.py:24
  51.5 80.3 %collective-permute-start.7 = (bf16[2,4,1,64,128]{4,3,2,1,0:T(8,128)(2,1)}, bf16[2,4,1,64,128]{4,3,2,1,0:T(8,128)(2,1)S(1)}, u32[]{:S(2)}, u32[]{:S(2)}) collective-permute-start(bf16[2,4,1,64,128]{4,3,2,1,0:T(8,128)(2,1)} %get-tuple-element.49), channel_id=1, source_target_pairs={{1,0},{2,1},{3,2},{5,4},{6,5},{7,6},{9,8},{10,9},{11,10},{13,12},{... | collective-permute-start | bytes 393224 | tf_op jit(solution)/shard_map/ppermute | solution.py:26
  54.7 77.1 %copy-start.3 = (bf16[2,4,8,64,128]{4,3,2,1,0:T(8,128)(2,1)S(1)}, bf16[2,4,8,64,128]{4,3,2,1,0:T(8,128)(2,1)}, u32[]{:S(2)}) copy-start(bf16[2,4,8,64,128]{4,3,2,1,0:T(8,128)(2,1)} %copy-done.2) | copy-start | bytes 3145732
  131.8 0.7 copy-start
  131.8 0.7 copy-start.1
  307.7 6.0 %copy-start.4 = (f32[9,3,64,32]{2,1,3,0:T(4,128)S(1)}, f32[9,3,64,32]{2,1,3,0:T(4,128)}, u32[]{:S(2)}) copy-start(f32[9,3,64,32]{2,1,3,0:T(4,128)} %all-reduce.6.cloned.1.call-done) | copy-start | bytes 663556
  313.7 1.0 copy-start.5
Sparse Core Ops, SparseCore 0:
  177.4 130.3 all-reduce.5

commit v2 on v1

--- a/solution.py
+++ b/solution.py
@@ -30,6 +30,35 @@
     return cells
 
 
+def swapped_sum(u, axis):
+    count = lax.axis_size(axis)
+    if count & (count - 1):
+        return lax.psum(u, axis)
+    step = 1
+    while step < count:
+        u = u + lax.ppermute(u, axis, [(i, i ^ step) for i in range(count)])
+        step *= 2
+    return u
+
+
+def swapped(u, axis):
+    return lax.ppermute(u, axis, [(0, 1), (1, 0)])
+
+
+def total_sum(u):
+    if lax.axis_size("dp") != 2:
+        return lax.psum(u, ("dp", "gx", "gy"))
+    half = u.shape[0] // 2
+    me = lax.axis_index("dp")
+    mine = lax.dynamic_slice_in_dim(u, me * half, half, 0)
+    other = lax.dynamic_slice_in_dim(u, (1 - me) * half, half, 0)
+    mine = mine + swapped(other, "dp")
+    mine = swapped_sum(swapped_sum(mine, "gx"), "gy")
+    other = swapped(mine, "dp")
+    first = me == 0
+    return jnp.concatenate([jnp.where(first, mine, other), jnp.where(first, other, mine)], axis=0)
+
+
 def silu_parts(z):
     s = 1.0 / (1.0 + jnp.exp(-z))
     return (z * s, s * (1.0 + z * (1.0 - s)), s * (1.0 - s) * (2.0 + z * (1.0 - 2.0 * s)))
@@ -63,7 +92,7 @@
     return from_left(y[:n]) + y[n : 2 * n] + from_right(y[2 * n : 3 * n])
 
 
-def forward_kernel(v_ref, l1_ref, b1_ref, l2_ref, b2_ref, pq_ref, a_ref, ta_ref, d_ref, pool_ref, tpool_ref):
+def forward_kernel(v_ref, l1_ref, b1_ref, l2_ref, b2_ref, pq_ref, a_ref, ta_ref, d_ref, pool_ref):
     nx, ny, lanes = (pq_ref.shape[1], pq_ref.shape[2], pq_ref.shape[4])
     b1 = b1_ref[...]
     l1 = l1_ref[...]
@@ -97,20 +126,20 @@
                 ttotal = ttotal + slope * t2
                 pq_ref[0, x, y + k] = slope.astype(BF16)
                 pq_ref[1, x, y + k] = (bend * t2).astype(BF16)
-    pool_ref[...] = jnp.sum(total, axis=1, keepdims=True)
-    tpool_ref[...] = jnp.sum(ttotal, axis=1, keepdims=True)
+    both = (jnp.sum(total, axis=1, keepdims=True), jnp.sum(ttotal, axis=1, keepdims=True))
+    pool_ref[...] = jnp.where(lane_of(pool_ref.shape) == 0, both[0], both[1])
 
 
 NT = (((1,), (1,)), ((), ()))
 
 
 def backward_kernel(
-    cells, batch, pq_ref, a_ref, ta_ref, d_ref, v_ref, lb_ref, pool_ref, tpool_ref, targets_ref,
-    head_w_ref, head_b_ref, dir_head_ref, h2_ref, h1_ref, hd_ref, field_ref, g_ref, tg_ref, t1_ref,
+    cells, batch, pq_ref, a_ref, ta_ref, d_ref, v_ref, lb_ref, pool_ref, targets_ref,
+    head_w_ref, head_b_ref, dir_head_ref, h_ref, hd_ref, field_ref, g_ref, tg_ref,
 ):
     nx, ny, lanes = (d_ref.shape[1], d_ref.shape[2], d_ref.shape[4])
-    pooled = pool_ref[...] / cells
-    tpooled = tpool_ref[...] / cells
+    pooled = pool_ref[:, 0:1] / cells
+    tpooled = pool_ref[:, 1:2] / cells
     head_w = head_w_ref[...]
     dir_head = dir_head_ref[...]
     out = jnp.sum(pooled * head_w, axis=0, keepdims=True) + head_b_ref[...]
@@ -134,14 +163,22 @@
             columns.append(jnp.concatenate([from_right(u), u, from_left(u)], axis=0).astype(BF16))
         return jnp.concatenate(columns, axis=1)
 
-    h2 = jnp.zeros(h2_ref.shape, F32)
+    cut = 8 * C1
+    most = jnp.zeros((3 * C2, cut), F32)
+    rest = jnp.zeros((C1, 3 * C2), F32)
     for x in range(nx):
         for y in range(0, ny, 2):
-            h2 = h2 + lax.dot_general(moved(tg_ref, x, y), window(a_ref, x, y, 2), NT, preferred_element_type=F32)
-            h2 = h2 + lax.dot_general(moved(g_ref, x, y), window(ta_ref, x, y, 2), NT, preferred_element_type=F32)
-    h2_ref[...] = h2
+            for grads, cells_ref in ((tg_ref, a_ref), (g_ref, ta_ref)):
+                g = moved(grads, x, y)
+                u = window(cells_ref, x, y, 2)
+                most = most + lax.dot_general(g, u[:cut], NT, preferred_element_type=F32)
+                rest = rest + lax.dot_general(u[cut:], g, NT, preferred_element_type=F32)
+    top = 3 * C2
+    h_ref[:top, :] = most
+    h_ref[top:, :] = jnp.zeros((2 * C1, cut), F32)
+    h_ref[top : top + C1, : 3 * C2] = rest
     n = 3 * C1
-    h1 = jnp.zeros(h1_ref.shape, F32)
+    h1 = jnp.zeros((C1, 9 * ROWS), F32)
     for x in range(nx):
         for y in range(0, ny, 2):
             res = jnp.dot(lb_ref[...], window(g_ref, x, y, 2), preferred_element_type=F32)
@@ -155,7 +192,7 @@
             h1 = h1 + lax.dot_general(
                 jnp.concatenate(grads, axis=1), window(v_ref, x + 1, y + 1, 2), NT, preferred_element_type=F32
             )
-    h1_ref[...] = h1
+    h_ref[top + C1 :, : 9 * ROWS] = h1
 
 
 def vmem_call(kernel, shapes, scratch=()):
@@ -187,41 +224,42 @@
     l2 = second.transpose(0, 2, 3, 1, 4).reshape(6 * C2, 9 * C1)
     lb = jnp.flip(second, (1, 2)).transpose(0, 2, 4, 1, 3).reshape(6 * C1, 9 * C2)
     shape = jax.ShapeDtypeStruct
-    pq, a1, ta1, d, pool, tpool = vmem_call(
+    pq, a1, ta1, d, pool = vmem_call(
         forward_kernel,
         (
             shape((2, nx, ny, C2, lanes), BF16),
             shape((nx + 2, ny + 2, C1, lanes), BF16),
             shape((nx + 2, ny + 2, C1, lanes), BF16),
             shape((2, nx, ny, C1, lanes), BF16),
-            shape((C2, 1), F32),
-            shape((C2, 1), F32),
+            shape((C2, 2), F32),
         ),
     )(v, l1, conv1_b[:, None], l2, conv2_b[:, None])
-    pool, tpool = lax.psum((pool, tpool), ("gx", "gy"))
+    pool = swapped_sum(swapped_sum(pool, "gx"), "gy")
     pq = extended(pq, (("gx", 1), ("gy", 2)), 1)
 
     def backward(*refs):
         backward_kernel(cells, batch, *refs)
 
-    h2, h1, hd, field = vmem_call(
+    h, hd, field = vmem_call(
         backward,
         (
-            shape((3 * C2, 9 * C1), F32),
-            shape((C1, 9 * ROWS), F32),
+            shape((3 * C2 + 2 * C1, 8 * C1), F32),
             shape((C2, head_w.shape[1]), F32),
             shape((C1, nx, ny, lanes), F32),
         ),
         (
             pltpu.VMEM((nx + 2, ny + 2, C2, lanes), BF16),
             pltpu.VMEM((nx + 2, ny + 2, C2, lanes), BF16),
-            pltpu.VMEM((8, lanes), F32),
         ),
-    )(pq, a1, ta1, d, v, lb, pool, tpool, targets, head_w, head_b[None], dir_head)
-    leader = ((lax.axis_index("gx") == 0) & (lax.axis_index("gy") == 0)).astype(F32)
-    h2, h1, hd = lax.psum((h2, h1, leader * hd), ("dp", "gx", "gy"))
-    h2 = h2.reshape(3, C2, 9, C1).transpose(2, 0, 1, 3).reshape(27, C2 * C1)
-    h1 = h1.reshape(C1, 9, ROWS)[:, :, : 3 * C0].reshape(C1, 27, C0).transpose(1, 0, 2).reshape(27, C1 * C0)
+    )(pq, a1, ta1, d, v, lb, pool, targets, head_w, head_b[None], dir_head)
+    hd = swapped_sum(hd, "dp")
+    h = total_sum(h)
+    top = 3 * C2
+    most = h[:top].reshape(3, C2, 8, C1).transpose(2, 0, 1, 3).reshape(24, C2 * C1)
+    rest = h[top : top + C1, :top].reshape(C1, 3, C2).transpose(1, 2, 0).reshape(3, C2 * C1)
+    h2 = jnp.concatenate([most, rest], axis=0)
+    h1 = h[top + C1 :, : 9 * ROWS].reshape(C1, 9, ROWS)[:, :, : 3 * C0]
+    h1 = h1.reshape(C1, 27, C0).transpose(1, 0, 2).reshape(27, C1 * C0)
     quad = jnp.sum(dir1 * h1) + jnp.sum(dir2 * h2) + jnp.sum(dir_head * hd)
     length = jnp.sum(dir1 * dir1) + jnp.sum(dir2 * dir2) + jnp.sum(dir_head * dir_head)
     nrm = jnp.sqrt(jnp.sum(h1 * h1) + jnp.sum(h2 * h2) + jnp.sum(hd * hd) + 1e-06)

time: 329 us -> 103 us (0.31)
  blocking collectives: 113 us -> 0 us
  waiting for transfers between devices: 142 us -> 35 us
  between operations: 21.4 us -> 8.02 us
  starting transfers between devices: 22.5 us -> 34.1 us
    psum x1 -> x0, waiting for transfers between devices: 130 us -> none  [per_device(): h2, h1, hd = lax.psum((h2, h1, leader * hd), ('dp', 'gx', 'gy'))]
    psum x2 -> x0, blocking collectives: 113 us -> none  [the longest x1 74.8 us: per_device(): pool, tpool = lax.psum((pool, tpool), ('gx', 'gy'))]
    ppermute x0 -> x11, waiting for transfers between devices: none -> 32.2 us  [the longest x9 30.1 us: swapped_sum(): u = u + lax.ppermute(u, axis, [(i, i ^ step) for i in range(count)])]
    ppermute x0 -> x11, starting transfers between devices: none -> 11.7 us  [the longest x9 11.5 us: swapped_sum(): u = u + lax.ppermute(u, axis, [(i, i ^ step) for i in range(count)])]
    ppermute x4, waiting for transfers between devices: 9.28 us -> 2.76 us  [extended(): lax.ppermute(head, axis, [((i + 1) % count, i) for i in range(ends)])]
  transfers between devices with their start and end apart: 9 -> 19, of which waited for: 4 -> 10; matrix products, arithmetic and copies ran while one was open for 4% -> 11% of each run, Pallas kernels for 0% -> 0%
where the time goes in v2:
time: 103 us
  waiting for transfers between devices  35 us (34%)
  starting transfers between devices  34.1 us (33%)
  local copies, waits for them, and re-layouts  11.2 us (11%)
  between operations  8.02 us (8%)
  other arithmetic  8 us (8%)
  Pallas kernels  6.19 us (6%)
    ppermute x9, waiting for transfers between devices, swapped_sum(): u = u + lax.ppermute(u, axis, [(i, i ^ step) for i in range(count)])  30.1 us
    ppermute x4, starting transfers between devices, extended(): lax.ppermute(tail, axis, [(i, (i + 1) % count) for i in range(ends)])  17.3 us
    ppermute x9, starting transfers between devices, swapped_sum(): u = u + lax.ppermute(u, axis, [(i, i ^ step) for i in range(count)])  11.5 us
    ppermute x4, starting transfers between devices, extended(): lax.ppermute(head, axis, [((i + 1) % count, i) for i in range(ends)])  5.17 us
    pallas_call x1, Pallas kernels, per_device(): vmem_call(backward, (shape((3 * C2 + 2 * C1, 8 * C1), F32), shape((C2, he...  4.21 us
    unnamed x30, local copies, waits for them, and re-layouts  2.82 us
    ppermute x4, waiting for transfers between devices, extended(): lax.ppermute(head, axis, [((i + 1) % count, i) for i in range(ends)])  2.76 us
    another operation x4, local copies, waits for them, and re-layouts, per_device(): first = jnp.stack((conv1_w, dir1.astype(BF16))).reshape(2, 9, 3, C1, C0)  2.15 us
  transfers between devices with their start and end apart: 19, of which 10 were waited for; matrix products, arithmetic and copies ran while one was open for 11% of the time, Pallas kernels for 0%

profile of v2, /device:TPU:0, one launch (start us, length us, event | category | flops | bytes accessed | tf_op | source)
XLA Modules:
  0.0 102.5 jit_solution(13493882081988508141)
XLA Ops:
  0.6 0.8 copy.71
  1.6 1.3 %collective-permute-start.1 = (bf16[2,8,16,128]{3,2,1,0:T(8,128)(2,1)S(1)}, bf16[2,8,16,128]{3,2,1,0:T(8,128)(2,1)S(1)}, u32[]{:S(2)}, u32[]{:S(2)}) collective-permute-start(bf16[2,8,16,128]{3,2,1,0:T(8,128)(2,1)S(1)} %concatenate.23), channel_id=1, source_target_pairs={{4,0},{8,4},{12,8},{5,1},{9,5},{13,9},{6,2},{10,6},{14,10},{7,3},{... | collective-permute-start | bytes 196616 | tf_op jit(solution)/shard_map/ppermute | solution.py:26
  2.9 5.5 %collective-permute-start = (bf16[2,8,16,128]{3,2,1,0:T(8,128)(2,1)S(1)}, bf16[2,8,16,128]{3,2,1,0:T(8,128)(2,1)S(1)}, u32[]{:S(2)}, u32[]{:S(2)}) collective-permute-start(bf16[2,8,16,128]{3,2,1,0:T(8,128)(2,1)S(1)} %concatenate.23), channel_id=1, source_target_pairs={{0,4},{4,8},{8,12},{1,5},{5,9},{9,13},{2,6},{6,10},{10,14},{3,7},{... | collective-permute-start | bytes 196616 | tf_op jit(solution)/shard_map/ppermute | solution.py:24
  8.4 1.4 %multiply_reduce_fusion.7 = (f32[]{:T(128)}, bf16[27,128]{1,0:T(8,128)(2,1)S(1)}) fusion(f32[27,128]{1,0:T(8,128)} %param.19), kind=kLoop, calls=%fused_computation.30 | loop fusion | flops 10367 | bytes 20740 | tf_op jit(solution)/shard_map/reduce_sum | solution.py:264
  9.8 1.0 convert_element_type.11
  11.5 1.2 %stack.18 = bf16[1,9,3,32,4]{4,3,2,1,0:T(8,128)(2,1)S(1)} reshape(bf16[27,128]{1,0:T(8,128)(2,1)} %param.13) | data formatting | bytes 13824 | tf_op jit(solution)/shard_map/stack | solution.py:220
  13.8 4.0 %collective-permute-start.2 = (bf16[6,2,16,128]{3,2,1,0:T(8,128)(2,1)S(1)}, bf16[6,2,16,128]{3,2,1,0:T(8,128)(2,1)S(1)}, u32[]{:S(2)}, u32[]{:S(2)}) collective-permute-start(bf16[6,2,16,128]{3,2,1,0:T(8,128)(2,1)S(1)} %get-tuple-element.48), channel_id=1, source_target_pairs={{0,1},{1,2},{2,3},{4,5},{5,6},{6,7},{8,9},{9,10},{10,11},{12,13},{... | collective-permute-start | bytes 147464 | tf_op jit(solution)/shard_map/ppermute | solution.py:24
  17.8 1.3 %collective-permute-start.3 = (bf16[6,2,16,128]{3,2,1,0:T(8,128)(2,1)S(1)}, bf16[6,2,16,128]{3,2,1,0:T(8,128)(2,1)S(1)}, u32[]{:S(2)}, u32[]{:S(2)}) collective-permute-start(bf16[6,2,16,128]{3,2,1,0:T(8,128)(2,1)S(1)} %get-tuple-element.49), channel_id=1, source_target_pairs={{1,0},{2,1},{3,2},{5,4},{6,5},{7,6},{9,8},{10,9},{11,10},{13,12},{... | collective-permute-start | bytes 147464 | tf_op jit(solution)/shard_map/ppermute | solution.py:26
  19.6 0.7 copy.53
  21.0 2.8 %collective-permute-done.3 = bf16[6,2,16,128]{3,2,1,0:T(8,128)(2,1)S(1)} collective-permute-done((bf16[6,2,16,128]{3,2,1,0:T(8,128)(2,1)S(1)}, bf16[6,2,16,128]{3,2,1,0:T(8,128)(2,1)S(1)}, u32[]{:S(2)}, u32[]{:S(2)}) %collective-permute-start.3) | collective-permute-done | bytes 49184 | tf_op jit(solution)/shard_map/ppermute | solution.py:26
  23.8 2.0 %shard_map.146 = (bf16[2,2,8,64,128]{4,3,2,1,0:T(8,128)(2,1)S(1)}, bf16[4,10,32,128]{3,2,1,0:T(8,128)(2,1)S(1)}, bf16[4,10,32,128]{3,2,1,0:T(8,128)(2,1)S(1)}, b...) custom-call(bf16[6,12,16,128]{3,2,1,0:T(8,128)(2,1)S(1)} %pad_maximum_fusion.1.v_ref.refs_4_, ...), custom_call_target="tpu_custom_call" | custom-call | tf_op jit(solution)/shard_map/pallas_call | solution.py:227
  25.9 4.3 %collective-permute-start.4 = (bf16[2,1,8,64,128]{4,3,2,1,0:T(8,128)(2,1)S(1)}, bf16[2,1,8,64,128]{4,3,2,1,0:T(8,128)(2,1)S(1)}, u32[]{:S(2)}, u32[]{:S(2)}) collective-permute-start(bf16[2,1,8,64,128]{4,3,2,1,0:T(8,128)(2,1)S(1)} %get-tuple-element.45), channel_id=1, source_target_pairs={{0,4},{4,8},{8,12},{1,5},{5,9},{9,13},{2,6},{6,10},{10,14},{3,7},{... | collective-permute-start | bytes 786440 | tf_op jit(solution)/shard_map/ppermute | solution.py:24
  30.2 1.3 %collective-permute-start.5 = (bf16[2,1,8,64,128]{4,3,2,1,0:T(8,128)(2,1)S(1)}, bf16[2,1,8,64,128]{4,3,2,1,0:T(8,128)(2,1)S(1)}, u32[]{:S(2)}, u32[]{:S(2)}) collective-permute-start(bf16[2,1,8,64,128]{4,3,2,1,0:T(8,128)(2,1)S(1)} %get-tuple-element.44), channel_id=1, source_target_pairs={{4,0},{8,4},{12,8},{5,1},{9,5},{13,9},{6,2},{10,6},{14,10},{7,3},{... | collective-permute-start | bytes 786440 | tf_op jit(solution)/shard_map/ppermute | solution.py:26
  31.5 2.7 %collective-permute-start.8 = (f32[64,2]{1,0:T(8,128)S(1)}, f32[64,2]{1,0:T(8,128)S(1)}, u32[]{:S(2)}, u32[]{:S(2)}) collective-permute-start(f32[64,2]{1,0:T(8,128)S(1)} %get-tuple-element.17), channel_id=1, source_target_pairs={{0,4},{4,0},{8,12},{12,8},{1,5},{5,1},{9,13},{13,9},{2,6},{6,2},{1... | collective-permute-start | bytes 1544 | tf_op jit(solution)/shard_map/ppermute | solution.py:39
  34.2 7.2 %collective-permute-done.8 = f32[64,2]{1,0:T(8,128)S(1)} collective-permute-done((f32[64,2]{1,0:T(8,128)S(1)}, f32[64,2]{1,0:T(8,128)S(1)}, u32[]{:S(2)}, u32[]{:S(2)}) %collective-permute-start.8) | collective-permute-done | bytes 544 | tf_op jit(solution)/shard_map/ppermute | solution.py:39
  42.3 3.5 %collective-permute-start.6 = (bf16[2,4,1,64,128]{4,3,2,1,0:T(8,128)(2,1)}, bf16[2,4,1,64,128]{4,3,2,1,0:T(8,128)(2,1)S(1)}, u32[]{:S(2)}, u32[]{:S(2)}) collective-permute-start(bf16[2,4,1,64,128]{4,3,2,1,0:T(8,128)(2,1)} %get-tuple-element.42), channel_id=1, source_target_pairs={{0,1},{1,2},{2,3},{4,5},{5,6},{6,7},{8,9},{9,10},{10,11},{12,13},{... | collective-permute-start | bytes 393224 | tf_op jit(solution)/shard_map/ppermute | solution.py:24
  45.8 1.3 %collective-permute-start.7 = (bf16[2,4,1,64,128]{4,3,2,1,0:T(8,128)(2,1)}, bf16[2,4,1,64,128]{4,3,2,1,0:T(8,128)(2,1)S(1)}, u32[]{:S(2)}, u32[]{:S(2)}) collective-permute-start(bf16[2,4,1,64,128]{4,3,2,1,0:T(8,128)(2,1)} %get-tuple-element.43), channel_id=1, source_target_pairs={{1,0},{2,1},{3,2},{5,4},{6,5},{7,6},{9,8},{10,9},{11,10},{13,12},{... | collective-permute-start | bytes 393224 | tf_op jit(solution)/shard_map/ppermute | solution.py:26
  47.2 2.7 %collective-permute-start.10 = (f32[64,2]{1,0:T(8,128)S(1)}, f32[64,2]{1,0:T(8,128)S(1)}, u32[]{:S(2)}, u32[]{:S(2)}) collective-permute-start(f32[64,2]{1,0:T(8,128)S(1)} %add.62), channel_id=1, source_target_pairs={{0,1},{1,0},{2,3},{3,2},{4,5},{5,4},{6,7},{7,6},{8,9},{9,8},{10,11... | collective-permute-start | bytes 1544 | tf_op jit(solution)/shard_map/ppermute | solution.py:39
  49.9 3.6 %collective-permute-done.10 = f32[64,2]{1,0:T(8,128)S(1)} collective-permute-done((f32[64,2]{1,0:T(8,128)S(1)}, f32[64,2]{1,0:T(8,128)S(1)}, u32[]{:S(2)}, u32[]{:S(2)}) %collective-permute-start.10) | collective-permute-done | bytes 544 | tf_op jit(solution)/shard_map/ppermute | solution.py:39
  53.5 1.5 %collective-permute-start.11 = (f32[64,2]{1,0:T(8,128)S(1)}, f32[64,2]{1,0:T(8,128)S(1)}, u32[]{:S(2)}, u32[]{:S(2)}) collective-permute-start(f32[64,2]{1,0:T(8,128)S(1)} %add.63), channel_id=1, source_target_pairs={{0,2},{1,3},{2,0},{3,1},{4,6},{5,7},{6,4},{7,5},{8,10},{9,11},{10,... | collective-permute-start | bytes 1544 | tf_op jit(solution)/shard_map/ppermute | solution.py:39
  55.3 0.8 copy.58
  56.5 1.9 %collective-permute-done.11 = f32[64,2]{1,0:T(8,128)S(1)} collective-permute-done((f32[64,2]{1,0:T(8,128)S(1)}, f32[64,2]{1,0:T(8,128)S(1)}, u32[]{:S(2)}, u32[]{:S(2)}) %collective-permute-start.11) | collective-permute-done | bytes 544 | tf_op jit(solution)/shard_map/ppermute | solution.py:39
  58.5 1.4 %pad_maximum_fusion.refs_0_ = bf16[2,4,10,64,128]{4,3,2,1,0:T(8,128)(2,1)S(1)} fusion(bf16[2,4,1,64,128]{4,3,2,1,0:T(8,128)(2,1)S(1)} %collective-permute-done.7, bf16[2,4,8,64,128]{4,3,2,1,0:T(8,128)(2,1)} %copy-done.2, bf16[2,4,1,64,128]{4,3,2,1,0:T(8,128)(2,1)S(1)} %collective-permute-done.6), kind=kLoop, calls=%fused_computation | loop fusion | flops 1310720 | bytes 2621440 | tf_op jit(solution)/shard_map/concatenate | solution.py:22
  59.9 4.2 %shard_map.147 = (f32[256,256]{1,0:T(8,128)S(1)}, f32[64,4]{1,0:T(8,128)S(1)}, f32[32,2,8,128]{3,2,1,0:T(8,128)}) custom-call(bf16[2,4,10,64,128]{4,3,2,1,0:T(8,128)(2,1)S(1)} %pad_maximum_fusion.refs_0_, bf16[4,10,32,128]{3,2,1,0:T(8,128)(2,1)S(1)} %get-tuple-element.14.refs_1_, bf16[4,10,32,128]{3,2,1,0:T(8,128)(2,1)S(1)} %get-tuple-element.15.refs_2_, ...), custom_call_target="tpu_custom_call" | custom-call | tf_op jit(solution)/shard_map/pallas_call | solution.py:243
  64.2 1.3 %collective-permute-done.12 = f32[128,256]{1,0:T(8,128)S(1)} collective-permute-done((f32[128,256]{1,0:T(8,128)S(1)}, f32[128,256]{1,0:T(8,128)S(1)}, u32[]{:S(2)}, u32[]{:S(2)}) %collective-permute-start.12) | collective-permute-done | bytes 131104 | tf_op jit(solution)/shard_map/ppermute | solution.py:45
  66.2 4.9 %collective-permute-done.13 = f32[128,256]{1,0:T(8,128)S(1)} collective-permute-done((f32[128,256]{1,0:T(8,128)S(1)}, f32[128,256]{1,0:T(8,128)S(1)}, u32[]{:S(2)}, u32[]{:S(2)}) %collective-permute-start.13) | collective-permute-done | bytes 131104 | tf_op jit(solution)/shard_map/ppermute | solution.py:39
  71.2 2.1 %collective-permute-start.14 = (f32[128,256]{1,0:T(8,128)S(1)}, f32[128,256]{1,0:T(8,128)S(1)}, u32[]{:S(2)}, u32[]{:S(2)}) collective-permute-start(f32[128,256]{1,0:T(8,128)S(1)} %add.68), channel_id=1, source_target_pairs={{0,8},{4,12},{8,0},{12,4},{1,9},{5,13},{9,1},{13,5},{2,10},{6,14},... | collective-permute-start | bytes 393224 | tf_op jit(solution)/shard_map/ppermute | solution.py:39
  73.3 3.0 %collective-permute-done.14 = f32[128,256]{1,0:T(8,128)S(1)} collective-permute-done((f32[128,256]{1,0:T(8,128)S(1)}, f32[128,256]{1,0:T(8,128)S(1)}, u32[]{:S(2)}, u32[]{:S(2)}) %collective-permute-start.14) | collective-permute-done | bytes 131104 | tf_op jit(solution)/shard_map/ppermute | solution.py:39
  76.6 4.8 %collective-permute-done.15 = f32[128,256]{1,0:T(8,128)S(1)} collective-permute-done((f32[128,256]{1,0:T(8,128)S(1)}, f32[128,256]{1,0:T(8,128)S(1)}, u32[]{:S(2)}, u32[]{:S(2)}) %collective-permute-start.15) | collective-permute-done | bytes 131104 | tf_op jit(solution)/shard_map/ppermute | solution.py:39
  81.3 1.5 %collective-permute-start.16 = (f32[128,256]{1,0:T(8,128)S(1)}, f32[128,256]{1,0:T(8,128)S(1)}, u32[]{:S(2)}, u32[]{:S(2)}) collective-permute-start(f32[128,256]{1,0:T(8,128)S(1)} %add.70), channel_id=1, source_target_pairs={{0,2},{1,3},{2,0},{3,1},{4,6},{5,7},{6,4},{7,5},{8,10},{9,11},{10,... | collective-permute-start | bytes 393224 | tf_op jit(solution)/shard_map/ppermute | solution.py:39
  83.6 4.8 %collective-permute-done.16 = f32[128,256]{1,0:T(8,128)S(1)} collective-permute-done((f32[128,256]{1,0:T(8,128)S(1)}, f32[128,256]{1,0:T(8,128)S(1)}, u32[]{:S(2)}, u32[]{:S(2)}) %collective-permute-start.16) | collective-permute-done | bytes 131104 | tf_op jit(solution)/shard_map/ppermute | solution.py:39
  92.3 0.7 multiply_reduce_fusion
  (102 shorter events, 13.1 us)
Async XLA Ops:
  0.6 12.7 %copy-start.4 = (bf16[27,2048]{1,0:T(8,128)(2,1)S(1)}, bf16[27,2048]{1,0:T(8,128)(2,1)}, u32[]{:S(2)}) copy-start(bf16[27,2048]{1,0:T(8,128)(2,1)} %param.15) | copy-start | bytes 331780
  1.6 12.1 %collective-permute-start.1 = (bf16[2,8,16,128]{3,2,1,0:T(8,128)(2,1)S(1)}, bf16[2,8,16,128]{3,2,1,0:T(8,128)(2,1)S(1)}, u32[]{:S(2)}, u32[]{:S(2)}) collective-permute-start(bf16[2,8,16,128]{3,2,1,0:T(8,128)(2,1)S(1)} %concatenate.23), channel_id=1, source_target_pairs={{4,0},{8,4},{12,8},{5,1},{9,5},{13,9},{6,2},{10,6},{14,10},{7,3},{... | collective-permute-start | bytes 196616 | tf_op jit(solution)/shard_map/ppermute | solution.py:26
  2.9 10.9 %collective-permute-start = (bf16[2,8,16,128]{3,2,1,0:T(8,128)(2,1)S(1)}, bf16[2,8,16,128]{3,2,1,0:T(8,128)(2,1)S(1)}, u32[]{:S(2)}, u32[]{:S(2)}) collective-permute-start(bf16[2,8,16,128]{3,2,1,0:T(8,128)(2,1)S(1)} %concatenate.23), channel_id=1, source_target_pairs={{0,4},{4,8},{8,12},{1,5},{5,9},{9,13},{2,6},{6,10},{10,14},{3,7},{... | collective-permute-start | bytes 196616 | tf_op jit(solution)/shard_map/ppermute | solution.py:24
  13.3 5.9 %copy-start.9 = (f32[32]{0:T(128)S(1)}, f32[32]{0:T(128)}, u32[]{:S(2)}) copy-start(f32[32]{0:T(128)} %param.14) | copy-start | bytes 388
  13.3 6.0 %copy-start.8 = (f32[64]{0:T(128)S(1)}, f32[64]{0:T(128)}, u32[]{:S(2)}) copy-start(f32[64]{0:T(128)} %param.16) | copy-start | bytes 772
  13.8 7.2 %collective-permute-start.2 = (bf16[6,2,16,128]{3,2,1,0:T(8,128)(2,1)S(1)}, bf16[6,2,16,128]{3,2,1,0:T(8,128)(2,1)S(1)}, u32[]{:S(2)}, u32[]{:S(2)}) collective-permute-start(bf16[6,2,16,128]{3,2,1,0:T(8,128)(2,1)S(1)} %get-tuple-element.48), channel_id=1, source_target_pairs={{0,1},{1,2},{2,3},{4,5},{5,6},{6,7},{8,9},{9,10},{10,11},{12,13},{... | collective-permute-start | bytes 147464 | tf_op jit(solution)/shard_map/ppermute | solution.py:24
  17.8 6.0 %collective-permute-start.3 = (bf16[6,2,16,128]{3,2,1,0:T(8,128)(2,1)S(1)}, bf16[6,2,16,128]{3,2,1,0:T(8,128)(2,1)S(1)}, u32[]{:S(2)}, u32[]{:S(2)}) collective-permute-start(bf16[6,2,16,128]{3,2,1,0:T(8,128)(2,1)S(1)} %get-tuple-element.49), channel_id=1, source_target_pairs={{1,0},{2,1},{3,2},{5,4},{6,5},{7,6},{9,8},{10,9},{11,10},{13,12},{... | collective-permute-start | bytes 147464 | tf_op jit(solution)/shard_map/ppermute | solution.py:26
  25.9 15.5 %collective-permute-start.4 = (bf16[2,1,8,64,128]{4,3,2,1,0:T(8,128)(2,1)S(1)}, bf16[2,1,8,64,128]{4,3,2,1,0:T(8,128)(2,1)S(1)}, u32[]{:S(2)}, u32[]{:S(2)}) collective-permute-start(bf16[2,1,8,64,128]{4,3,2,1,0:T(8,128)(2,1)S(1)} %get-tuple-element.45), channel_id=1, source_target_pairs={{0,4},{4,8},{8,12},{1,5},{5,9},{9,13},{2,6},{6,10},{10,14},{3,7},{... | collective-permute-start | bytes 786440 | tf_op jit(solution)/shard_map/ppermute | solution.py:24
  30.2 11.3 %collective-permute-start.5 = (bf16[2,1,8,64,128]{4,3,2,1,0:T(8,128)(2,1)S(1)}, bf16[2,1,8,64,128]{4,3,2,1,0:T(8,128)(2,1)S(1)}, u32[]{:S(2)}, u32[]{:S(2)}) collective-permute-start(bf16[2,1,8,64,128]{4,3,2,1,0:T(8,128)(2,1)S(1)} %get-tuple-element.44), channel_id=1, source_target_pairs={{4,0},{8,4},{12,8},{5,1},{9,5},{13,9},{6,2},{10,6},{14,10},{7,3},{... | collective-permute-start | bytes 786440 | tf_op jit(solution)/shard_map/ppermute | solution.py:26
  31.5 9.9 %collective-permute-start.8 = (f32[64,2]{1,0:T(8,128)S(1)}, f32[64,2]{1,0:T(8,128)S(1)}, u32[]{:S(2)}, u32[]{:S(2)}) collective-permute-start(f32[64,2]{1,0:T(8,128)S(1)} %get-tuple-element.17), channel_id=1, source_target_pairs={{0,4},{4,0},{8,12},{12,8},{1,5},{5,1},{9,13},{13,9},{2,6},{6,2},{1... | collective-permute-start | bytes 1544 | tf_op jit(solution)/shard_map/ppermute | solution.py:39
  41.4 5.8 %collective-permute-start.9 = (f32[64,2]{1,0:T(8,128)S(1)}, f32[64,2]{1,0:T(8,128)S(1)}, u32[]{:S(2)}, u32[]{:S(2)}) collective-permute-start(f32[64,2]{1,0:T(8,128)S(1)} %add.61), channel_id=1, source_target_pairs={{0,8},{4,12},{8,0},{12,4},{1,9},{5,13},{9,1},{13,5},{2,10},{6,14},... | collective-permute-start | bytes 1544 | tf_op jit(solution)/shard_map/ppermute | solution.py:39
  41.6 5.6 %copy-start.2 = (bf16[2,4,8,64,128]{4,3,2,1,0:T(8,128)(2,1)}, bf16[2,4,8,64,128]{4,3,2,1,0:T(8,128)(2,1)S(1)}, u32[]{:S(2)}) copy-start(bf16[2,4,8,64,128]{4,3,2,1,0:T(8,128)(2,1)S(1)} %constant_dynamic-update-slice_fusion.2) | copy-start | bytes 3145732
  41.6 13.5 %copy-start.6 = (f32[64,4]{0,1:T(4,128)S(1)}, f32[64,4]{0,1:T(4,128)}, u32[]{:S(2)}) copy-start(f32[64,4]{0,1:T(4,128)} %param.21) | copy-start | bytes 3076
  41.6 13.6 %copy-start.7 = (f32[64,4]{0,1:T(4,128)S(1)}, f32[64,4]{0,1:T(4,128)}, u32[]{:S(2)}) copy-start(f32[64,4]{0,1:T(4,128)} %param.17) | copy-start | bytes 3076
  42.3 16.1 %collective-permute-start.6 = (bf16[2,4,1,64,128]{4,3,2,1,0:T(8,128)(2,1)}, bf16[2,4,1,64,128]{4,3,2,1,0:T(8,128)(2,1)S(1)}, u32[]{:S(2)}, u32[]{:S(2)}) collective-permute-start(bf16[2,4,1,64,128]{4,3,2,1,0:T(8,128)(2,1)} %get-tuple-element.42), channel_id=1, source_target_pairs={{0,1},{1,2},{2,3},{4,5},{5,6},{6,7},{8,9},{9,10},{10,11},{12,13},{... | collective-permute-start | bytes 393224 | tf_op jit(solution)/shard_map/ppermute | solution.py:24
  45.8 12.7 %collective-permute-start.7 = (bf16[2,4,1,64,128]{4,3,2,1,0:T(8,128)(2,1)}, bf16[2,4,1,64,128]{4,3,2,1,0:T(8,128)(2,1)S(1)}, u32[]{:S(2)}, u32[]{:S(2)}) collective-permute-start(bf16[2,4,1,64,128]{4,3,2,1,0:T(8,128)(2,1)} %get-tuple-element.43), channel_id=1, source_target_pairs={{1,0},{2,1},{3,2},{5,4},{6,5},{7,6},{9,8},{10,9},{11,10},{13,12},{... | collective-permute-start | bytes 393224 | tf_op jit(solution)/shard_map/ppermute | solution.py:26
  47.2 6.3 %collective-permute-start.10 = (f32[64,2]{1,0:T(8,128)S(1)}, f32[64,2]{1,0:T(8,128)S(1)}, u32[]{:S(2)}, u32[]{:S(2)}) collective-permute-start(f32[64,2]{1,0:T(8,128)S(1)} %add.62), channel_id=1, source_target_pairs={{0,1},{1,0},{2,3},{3,2},{4,5},{5,4},{6,7},{7,6},{8,9},{9,8},{10,11... | collective-permute-start | bytes 1544 | tf_op jit(solution)/shard_map/ppermute | solution.py:39
  53.5 4.9 %collective-permute-start.11 = (f32[64,2]{1,0:T(8,128)S(1)}, f32[64,2]{1,0:T(8,128)S(1)}, u32[]{:S(2)}, u32[]{:S(2)}) collective-permute-start(f32[64,2]{1,0:T(8,128)S(1)} %add.63), channel_id=1, source_target_pairs={{0,2},{1,3},{2,0},{3,1},{4,6},{5,7},{6,4},{7,5},{8,10},{9,11},{10,... | collective-permute-start | bytes 1544 | tf_op jit(solution)/shard_map/ppermute | solution.py:39
  58.4 1.4 %copy-start = (f32[1,4]{1,0:T(1,128)S(1)}, f32[1,4]{1,0:T(1,128)}, u32[]{:S(2)}) copy-start(f32[1,4]{1,0:T(1,128)} %refs_7_.1) | copy-start | bytes 52
  58.4 1.4 %copy-start.1 = (f32[4]{0:T(128)S(1)}, f32[4]{0:T(128)}, u32[]{:S(2)}) copy-start(f32[4]{0:T(128)} %param.18) | copy-start | bytes 52
  64.1 19.4 %copy-start.5 = (f32[27,128]{1,0:T(8,128)S(1)}, f32[27,128]{1,0:T(8,128)}, u32[]{:S(2)}) copy-start(f32[27,128]{1,0:T(8,128)} %param.19) | copy-start | bytes 41476
  64.1 1.4 %collective-permute-start.12 = (f32[128,256]{1,0:T(8,128)S(1)}, f32[128,256]{1,0:T(8,128)S(1)}, u32[]{:S(2)}, u32[]{:S(2)}) collective-permute-start(f32[128,256]{1,0:T(8,128)S(1)} %constant_dynamic-slice_fusion), channel_id=1, source_target_pairs={{0,16},{16,0},{1,17},{17,1},{2,18},{18,2},{3,19},{19,3},{4,20},{20... | collective-permute-start | bytes 393224 | tf_op jit(solution)/shard_map/ppermute | solution.py:45
  65.6 5.6 %collective-permute-start.13 = (f32[128,256]{1,0:T(8,128)S(1)}, f32[128,256]{1,0:T(8,128)S(1)}, u32[]{:S(2)}, u32[]{:S(2)}) collective-permute-start(f32[128,256]{1,0:T(8,128)S(1)} %dynamic-slice_add_fusion), channel_id=1, source_target_pairs={{0,4},{4,0},{8,12},{12,8},{1,5},{5,1},{9,13},{13,9},{2,6},{6,2},{1... | collective-permute-start | bytes 393224 | tf_op jit(solution)/shard_map/ppermute | solution.py:39
  71.2 5.1 %collective-permute-start.14 = (f32[128,256]{1,0:T(8,128)S(1)}, f32[128,256]{1,0:T(8,128)S(1)}, u32[]{:S(2)}, u32[]{:S(2)}) collective-permute-start(f32[128,256]{1,0:T(8,128)S(1)} %add.68), channel_id=1, source_target_pairs={{0,8},{4,12},{8,0},{12,4},{1,9},{5,13},{9,1},{13,5},{2,10},{6,14},... | collective-permute-start | bytes 393224 | tf_op jit(solution)/shard_map/ppermute | solution.py:39
  76.3 5.0 %collective-permute-start.15 = (f32[128,256]{1,0:T(8,128)S(1)}, f32[128,256]{1,0:T(8,128)S(1)}, u32[]{:S(2)}, u32[]{:S(2)}) collective-permute-start(f32[128,256]{1,0:T(8,128)S(1)} %add.69), channel_id=1, source_target_pairs={{0,1},{1,0},{2,3},{3,2},{4,5},{5,4},{6,7},{7,6},{8,9},{9,8},{10,11... | collective-permute-start | bytes 393224 | tf_op jit(solution)/shard_map/ppermute | solution.py:39
  81.3 7.0 %collective-permute-start.16 = (f32[128,256]{1,0:T(8,128)S(1)}, f32[128,256]{1,0:T(8,128)S(1)}, u32[]{:S(2)}, u32[]{:S(2)}) collective-permute-start(f32[128,256]{1,0:T(8,128)S(1)} %add.70), channel_id=1, source_target_pairs={{0,2},{1,3},{2,0},{3,1},{4,6},{5,7},{6,4},{7,5},{8,10},{9,11},{10,... | collective-permute-start | bytes 393224 | tf_op jit(solution)/shard_map/ppermute | solution.py:39
  82.8 5.6 %collective-permute-start.18 = (f32[64,4]{1,0:T(8,128)S(1)}, f32[64,4]{1,0:T(8,128)S(1)}, u32[]{:S(2)}, u32[]{:S(2)}) collective-permute-start(f32[64,4]{1,0:T(8,128)S(1)} %get-tuple-element.19), channel_id=1, source_target_pairs={{0,16},{16,0},{1,17},{17,1},{2,18},{18,2},{3,19},{19,3},{4,20},{20... | collective-permute-start | bytes 3080 | tf_op jit(solution)/shard_map/ppermute | solution.py:39
  88.4 1.4 %collective-permute-start.17 = (f32[128,256]{1,0:T(8,128)S(1)}, f32[128,256]{1,0:T(8,128)S(1)}, u32[]{:S(2)}, u32[]{:S(2)}) collective-permute-start(f32[128,256]{1,0:T(8,128)S(1)} %add.71), channel_id=1, source_target_pairs={{0,16},{16,0},{1,17},{17,1},{2,18},{18,2},{3,19},{19,3},{4,20},{20... | collective-permute-start | bytes 393224 | tf_op jit(solution)/shard_map/ppermute | solution.py:45
  91.3 1.0 copy-start.3
